TPU v7x, 32 devices: a whole 2x2x4 slice. The times are simulated.
32 devices in a mesh: dp: 8 (over z, x), tensor: 4 (over y, core).
Axes of the slice: x: 2, y: 2, z: 4, core: 2. Of those that a mesh axis runs over, the one named last changes fastest.
Arguments:
- logits: bfloat16 [16, 128, 19456], P('dp', None, 'tensor'), may hold values from -110 to 290
- token_ids: int32 [16, 128], P('dp'), may hold values from 0 to 19455
- response_mask: int32 [16, 128], P('dp'), may hold values 0 or 1
- lengths: int32 [16], P('dp'), may hold values from 16 to 128
- prompt_of: int32 [16], P('dp'), may hold values from 0 to 1, as said below
- old_logprob: float32 [16, 128], P('dp'), may hold values from -14 to -10
- ref_logprob: bfloat16 [16, 128], P(None, 'dp'), may hold values from -14 to -10
- advantages: float32 [16, 128], P('dp'), may hold values from -8 to 8
- returns: float32 [16, 128], P('dp'), may hold values from -6 to 6
- critic_hidden: bfloat16 [16, 128, 5120], P(None, 'dp', 'tensor'), may hold values from -6 to 6
- value_weight: bfloat16 [5120], P('tensor'), may hold values from -0.078125 to 0.078125
Outputs:
- token_loss: float32 [16, 128], P('dp')
- critic_grad: bfloat16 [16, 128, 5120], P(None, 'dp', 'tensor')
Inputs may be any that keep to these rules, and one draw needn't show every extreme that they name: `prompt_of`: each of the 2 prompts is named by exactly 8 sequences.
All inputs are finite; a program needn't handle non-finite values. No bound on the sum of `response_mask` on one device may be relied on, other than what follows from the above.
Results may differ from a plain program's by a relative error of at most 0.001.
Values may be sent and summed in bfloat16 or wider, within the bound.
No kernel may reach another device: no remote copies, remote signals or barrier semaphores. Data moves between devices by JAX's collectives and lax.ppermute only.
A program may use at most 64 MiB of HBM per device.

v0:
```python
import jax
import jax.numpy as jnp
from jax import lax
from jax.sharding import PartitionSpec as P

RESPONSES = 8


def per_device(
    logits,
    token_ids,
    response_mask,
    lengths,
    prompt_of,
    old_logprob,
    ref_logprob,
    advantages,
    returns,
    critic_hidden,
    value_weight,
):
    highest = lax.Precision.HIGHEST
    seq_rows, seq_len, vocab_width = logits.shape
    all_seqs, tile_len, feat_count = critic_hidden.shape
    dp_size = lax.axis_size("dp")
    head_weight = value_weight.astype(jnp.float32)
    tile_rows = critic_hidden.reshape(all_seqs * tile_len, feat_count)
    local_part = jnp.dot(tile_rows, value_weight, preferred_element_type=jnp.float32).reshape(
        all_seqs, tile_len
    )
    partial_value, ref_rows = (
        lax.all_to_all(local_part, "dp", split_axis=0, concat_axis=1, tiled=True),
        lax.all_to_all(
            ref_logprob.astype(jnp.float32), "dp", split_axis=0, concat_axis=1, tiled=True
        ),
    )
    position = lax.broadcasted_iota(jnp.int32, (seq_rows, seq_len), 1)
    live_mask = (response_mask * (position < lengths[:, None]).astype(jnp.int32)).astype(
        jnp.float32
    )
    prompt_count = seq_rows * dp_size // RESPONSES
    prompt_hot = (
        prompt_of[:, None] == lax.broadcasted_iota(jnp.int32, (seq_rows, prompt_count), 1)
    ).astype(jnp.float32)
    seq_tokens = jnp.sum(live_mask, axis=1)
    seq_total = jnp.sum(live_mask * advantages, axis=1)
    seq_square = jnp.sum(live_mask * advantages * advantages, axis=1)
    moments = jnp.dot(jnp.stack([seq_tokens, seq_total, seq_square]), prompt_hot, precision=highest)
    count_all, total_all, square_all = lax.psum((moments[0], moments[1], moments[2]), "dp")
    count_floor = jnp.maximum(count_all, 1.0)
    prompt_mean = total_all / count_floor
    prompt_var = (square_all - prompt_mean * total_all) / count_floor
    row_mean = jnp.dot(prompt_hot, prompt_mean, precision=highest)
    row_scale = lax.rsqrt(jnp.dot(prompt_hot, prompt_var, precision=highest) + 1.0)
    whitened = (advantages - row_mean[:, None]) * row_scale[:, None]
    local_top = jnp.max(logits, axis=2).astype(jnp.float32)
    local_sum = jnp.sum(jnp.exp(logits.astype(jnp.float32) - local_top[:, :, None]), axis=2)
    vocab_start = lax.axis_index("tensor") * vocab_width
    shifted = token_ids - vocab_start
    in_shard = (shifted >= 0) & (shifted < vocab_width)
    clipped_ids = jnp.clip(shifted, 0, vocab_width - 1)
    picked = jnp.take_along_axis(logits, clipped_ids[:, :, None], axis=2)[:, :, 0].astype(
        jnp.float32
    )
    target_part = jnp.where(in_shard, picked, 0.0)
    row_max = lax.pmax(local_top, "tensor")
    rescaled = local_sum * jnp.exp(local_top - row_max)
    total_sum, target_logit, value_pred = lax.psum((rescaled, target_part, partial_value), "tensor")
    logprob = target_logit - (row_max + jnp.log(total_sum))
    prob_ratio = jnp.exp(jnp.clip(logprob - old_logprob, -20.0, 20.0))
    surrogate = jnp.maximum(-whitened * prob_ratio, -whitened * jnp.clip(prob_ratio, 0.8, 1.2))
    surrogate = jnp.where(whitened < 0.0, jnp.minimum(surrogate, -3.0 * whitened), surrogate)
    ref_drift = jnp.clip(ref_rows - logprob, -20.0, 20.0)
    penalty = jnp.clip(jnp.exp(ref_drift) - ref_drift - 1.0, -10.0, 10.0)
    value_error = value_pred - returns
    token_loss = live_mask * (surrogate + 0.1 * penalty + 0.25 * value_error * value_error)
    grad_coeff = 32.0 * live_mask * value_error
    returned = lax.all_to_all(grad_coeff, "dp", split_axis=1, concat_axis=0, tiled=True)
    critic_grad = (returned[:, :, None] * head_weight[None, None, :]).astype(jnp.bfloat16)
    return (token_loss, critic_grad)


def solution(mesh):
    in_specs = (
        P("dp", None, "tensor"),
        P("dp", None),
        P("dp", None),
        P("dp"),
        P("dp"),
        P("dp", None),
        P(None, "dp"),
        P("dp", None),
        P("dp", None),
        P(None, "dp", "tensor"),
        P("tensor"),
    )
    out_specs = (P("dp", None), P(None, "dp", "tensor"))
    return jax.shard_map(
        per_device, mesh=mesh, in_specs=in_specs, out_specs=out_specs, check_vma=False
    )
```

profile of v0, /device:TPU:0, one launch (start us, length us, event | category | flops | bytes accessed | tf_op | source)
XLA Modules:
  0.0 71.6 jit_solution(9083070051270361440)
XLA Ops:
  0.7 1.4 %convert.1 = f32[8,2,16]{2,1,0:T(2,128)} convert(bf16[8,2,16]{2,1,0:T(2,128)(2,1)} %bitcast.45) | non-fusion elementwise | flops 256 | bytes 1536 | tf_op jit(solution)/shard_map/all_to_all | solution.py:33
  2.1 7.3 %all-to-all-start = ((f32[8,2,16]{2,1,0:T(2,128)}), f32[8,2,16]{2,1,0:T(2,128)S(1)}, u32[]{:S(2)}, u32[]{:S(2)}) async-start(f32[8,2,16]{2,1,0:T(2,128)} %convert.1), calls=%async_computation | async-start | bytes 16384 | tf_op jit(solution)/shard_map/all_to_all | solution.py:33
  9.4 2.1 %reduce_max.9 = bf16[2,128]{1,0:T(2,128)(2,1)S(1)} reduce(bf16[2,128,4864]{2,1,0:T(8,128)(2,1)} %param.11, bf16[]{:T(256)} %constant.27.clone.1), dimensions={2}, to_apply=%region_7.0 | reduce | flops 1244928 | bytes 2490882 | tf_op jit(solution)/shard_map/reduce_max | solution.py:56
  11.6 6.6 %pmax.7 = f32[2,128]{1,0:T(2,128)S(1)} all-reduce(bf16[2,128]{1,0:T(2,128)(2,1)S(1)} %reduce_max.9), channel_id=1, replica_groups=mesh['dp'=8,'tensor'=4] {'tensor'}, use_global_device_ids=true, to_apply=%region_8.9 | all-reduce | flops 256 | bytes 1536 | tf_op jit(solution)/shard_map/pmax | solution.py:66
  18.2 1.0 %exponential_reduce_fusion = f32[2,128]{1,0:T(2,128)S(1)} fusion(bf16[2,128,4864]{2,1,0:T(8,128)(2,1)S(1)} %copy-done.1, f32[2,128]{1,0:T(2,128)S(1)} %convert_element_type.27), kind=kLoop, calls=%fused_computation.1 | loop fusion | flops 3735296 | bytes 2492416 | tf_op jit(solution)/shard_map/reduce_sum | solution.py:57
  19.3 1.5 %fusion.2 = f32[1,8,2,16]{3,0,2,1:T(1,128)} fusion(bf16[8,2,16,1280]{3,2,1,0:T(8,128)(2,1)S(1)} %bitcast.41, bf16[1280,1,1,1]{0,1,2,3:T(2,128)(2,1)S(1)} %reshape.68), kind=kOutput, calls=%fused_computation.7 | convolution fusion | flops 655360 | bytes 658944 | tf_op jit(solution)/shard_map/dot_general | solution.py:28
  20.8 2.8 %gather_fusion = bf16[256]{0:T(256)(128)(2,1)S(1)} fusion(bf16[2,128,4864]{2,1,0:T(8,128)(2,1)S(1)} %copy-done.1, s32[256]{0:T(256)S(1)} %fusion.18), kind=kCustom, calls=%fused_computation | custom fusion | bytes 4096 | tf_op jit(solution)/shard_map/jit(take_along_axis)/gather | solution.py:62
  23.6 5.4 %all-to-all-start.1 = ((f32[8,2,16]{2,1,0:T(2,128)}), f32[8,2,16]{2,1,0:T(2,128)S(1)}, u32[]{:S(2)}, u32[]{:S(2)}) async-start(f32[8,2,16]{2,1,0:T(2,128)} %bitcast.16), calls=%async_computation.1 | async-start | bytes 16384 | tf_op jit(solution)/shard_map/all_to_all | solution.py:32
  29.1 0.1 all_to_all.44
  29.1 6.4 %all-to-all-done.1 = f32[8,2,16]{2,1,0:T(2,128)S(1)} async-done(((f32[8,2,16]{2,1,0:T(2,128)}), f32[8,2,16]{2,1,0:T(2,128)S(1)}, u32[]{:S(2)}, u32[]{:S(2)}) %all-to-all-start.1) | async-done | bytes 1056 | tf_op jit(solution)/shard_map/all_to_all | solution.py:32
  35.5 0.1 all_to_all.47
  35.6 5.6 %all-reduce.1 = (f32[2,128]{1,0:T(2,128)S(1)}, f32[2,128]{1,0:T(2,128)S(1)}, f32[2,128]{1,0:T(2,128)S(1)}) all-reduce(f32[2,128]{1,0:T(2,128)S(1)} %and_select_fusion.1, f32[2,128]{1,0:T(2,128)S(1)} %exponential_multiply_fusion, f32[2,128]{1,0:T(2,128)S(1)} %all_to_all.47), channel_id=1, replica_groups=mesh['dp'=8,'tensor'=4] {'tensor'}, use_global_device_ids=true, to_apply=%region_6.0 | all-reduce | flops 768 | bytes 6144 | tf_op jit(solution)/shard_map/psum | solution.py:68
  41.4 0.1 multiply_reduce_fusion.1
  41.5 0.3 fusion.4
  41.8 0.2 slice_reduce_fusion.1
  42.0 17.7 %all-reduce = (f32[2]{0:T(128)S(1)}, f32[2]{0:T(128)S(1)}, f32[2]{0:T(128)S(1)}) all-reduce(f32[2]{0:T(128)S(1)} %get-tuple-element.5, f32[2]{0:T(128)S(1)} %get-tuple-element.6, f32[2]{0:T(128)S(1)} %get-tuple-element.4), channel_id=1, replica_groups=mesh['dp'=8,'tensor'=4] {'dp'}, use_global_device_ids=true, to_apply=%region_5.0 | all-reduce | flops 6 | bytes 48 | tf_op jit(solution)/shard_map/psum | solution.py:49
  59.7 0.2 convolution_bitcast_fusion.1
  59.9 0.2 fusion.1
  60.1 0.1 all_to_all.48
  60.2 0.6 copy.19
  60.8 3.3 %all-to-all-start.2 = ((f32[2,8,16]{2,0,1:T(2,128)}), f32[2,8,16]{2,0,1:T(2,128)S(1)}, u32[]{:S(2)}, u32[]{:S(2)}) async-start(f32[2,8,16]{2,0,1:T(2,128)} %copy.19), calls=%async_computation.2 | async-start | bytes 16384 | tf_op jit(solution)/shard_map/all_to_all | solution.py:78
  64.1 0.6 fusion.22
  64.8 5.8 %all-to-all-done.2 = f32[2,8,16]{2,0,1:T(2,128)S(1)} async-done(((f32[2,8,16]{2,0,1:T(2,128)}), f32[2,8,16]{2,0,1:T(2,128)S(1)}, u32[]{:S(2)}, u32[]{:S(2)}) %all-to-all-start.2) | async-done | bytes 1056 | tf_op jit(solution)/shard_map/all_to_all | solution.py:78
  70.6 1.0 %multiply_convert_fusion = bf16[16,16,1280]{2,1,0:T(8,128)(2,1)} fusion(f32[1280]{0:T(1024)S(1)} %convert_element_type.29, f32[16,16]{1,0:T(8,128)S(1)} %bitcast.42), kind=kLoop, calls=%fused_computation.2 | loop fusion | flops 655360 | bytes 661504 | tf_op jit(solution)/shard_map/convert_element_type | solution.py:79
  (35 shorter events, 0.2 us)
Async XLA Ops:
  0.6 18.6 %copy-start = (bf16[16,16,1280]{2,1,0:T(8,128)(2,1)S(1)}, bf16[16,16,1280]{2,1,0:T(8,128)(2,1)}, u32[]{:S(2)}) copy-start(bf16[16,16,1280]{2,1,0:T(8,128)(2,1)} %param.20) | copy-start | bytes 1966084
  0.6 17.6 %copy-start.1 = (bf16[2,128,4864]{2,1,0:T(8,128)(2,1)S(1)}, bf16[2,128,4864]{2,1,0:T(8,128)(2,1)}, u32[]{:S(2)}) copy-start(bf16[2,128,4864]{2,1,0:T(8,128)(2,1)} %param.11) | copy-start | bytes 7471108
  2.1 21.5 %all-to-all-start = ((f32[8,2,16]{2,1,0:T(2,128)}), f32[8,2,16]{2,1,0:T(2,128)S(1)}, u32[]{:S(2)}, u32[]{:S(2)}) async-start(f32[8,2,16]{2,1,0:T(2,128)} %convert.1), calls=%async_computation | async-start | bytes 16384 | tf_op jit(solution)/shard_map/all_to_all | solution.py:33
  9.4 9.8 %copy-start.2 = (bf16[1280]{0:T(1024)(128)(2,1)S(1)}, bf16[1280]{0:T(1024)(128)(2,1)}, u32[]{:S(2)}) copy-start(bf16[1280]{0:T(1024)(128)(2,1)} %param.21) | copy-start | bytes 7684
  9.4 9.8 %copy-start.3 = (s32[2,128]{1,0:T(2,128)S(1)}, s32[2,128]{1,0:T(2,128)}, u32[]{:S(2)}) copy-start(s32[2,128]{1,0:T(2,128)} %param.12) | copy-start | bytes 3076
  11.5 29.7 %copy-start.5 = (f32[2,128]{1,0:T(2,128)S(1)}, f32[2,128]{1,0:T(2,128)}, u32[]{:S(2)}) copy-start(f32[2,128]{1,0:T(2,128)} %param.19) | copy-start | bytes 3076
  11.5 29.7 %copy-start.6 = (s32[2,128]{1,0:T(2,128)S(1)}, s32[2,128]{1,0:T(2,128)}, u32[]{:S(2)}) copy-start(s32[2,128]{1,0:T(2,128)} %param.13) | copy-start | bytes 3076
  11.5 29.7 %copy-start.8 = (s32[2]{0:T(128)S(1)}, s32[2]{0:T(128)}, u32[]{:S(2)}) copy-start(s32[2]{0:T(128)} %param.14) | copy-start | bytes 28
  11.6 29.8 %copy-start.4 = (f32[2,128]{1,0:T(2,128)S(1)}, f32[2,128]{1,0:T(2,128)}, u32[]{:S(2)}) copy-start(f32[2,128]{1,0:T(2,128)} %param.18) | copy-start | bytes 3076
  11.6 29.9 %copy-start.9 = (s32[2]{0:T(128)S(1)}, s32[2]{0:T(128)}, u32[]{:S(2)}) copy-start(s32[2]{0:T(128)} %param.15) | copy-start | bytes 28
  11.6 52.5 %copy-start.7 = (f32[2,128]{1,0:T(2,128)S(1)}, f32[2,128]{1,0:T(2,128)}, u32[]{:S(2)}) copy-start(f32[2,128]{1,0:T(2,128)} %param.16) | copy-start | bytes 3076
  23.6 12.0 %all-to-all-start.1 = ((f32[8,2,16]{2,1,0:T(2,128)}), f32[8,2,16]{2,1,0:T(2,128)S(1)}, u32[]{:S(2)}, u32[]{:S(2)}) async-start(f32[8,2,16]{2,1,0:T(2,128)} %bitcast.16), calls=%async_computation.1 | async-start | bytes 16384 | tf_op jit(solution)/shard_map/all_to_all | solution.py:32
  60.8 9.8 %all-to-all-start.2 = ((f32[2,8,16]{2,0,1:T(2,128)}), f32[2,8,16]{2,0,1:T(2,128)S(1)}, u32[]{:S(2)}, u32[]{:S(2)}) async-start(f32[2,8,16]{2,0,1:T(2,128)} %copy.19), calls=%async_computation.2 | async-start | bytes 16384 | tf_op jit(solution)/shard_map/all_to_all | solution.py:78
where the time goes:
time: 71.9 us; the launch traced here: 71.6 us
  blocking collectives  30 us (42%)
  starting transfers between devices  16 us (22%)
  waiting for transfers between devices  12.2 us (17%)
  other arithmetic  6.42 us (9%)
  local copies, waits for them, and re-layouts  3.95 us (5%)
  matrix products  2.1 us (3%)
  between operations  0.83 us (1%)
    psum x1, blocking collectives, per_device(): lax.psum((moments[0], moments[1], moments[2]), 'dp')  17.7 us
    all_to_all x1, starting transfers between devices, per_device(): lax.all_to_all(ref_logprob.astype(jnp.float32), 'dp', split_axis=0, conca...  7.28 us
    pmax x1, blocking collectives, per_device(): row_max = lax.pmax(local_top, 'tensor')  6.63 us
    all_to_all x1, waiting for transfers between devices, per_device(): lax.all_to_all(local_part, 'dp', split_axis=0, concat_axis=1, tiled=True)  6.41 us
    all_to_all x1, waiting for transfers between devices, per_device(): lax.all_to_all(grad_coeff, 'dp', split_axis=1, concat_axis=0, tiled=True)  5.8 us
    psum x1, blocking collectives, per_device(): lax.psum((rescaled, target_part, partial_value), 'tensor')  5.64 us
    all_to_all x1, starting transfers between devices, per_device(): lax.all_to_all(local_part, 'dp', split_axis=0, concat_axis=1, tiled=True)  5.43 us
    all_to_all x1, starting transfers between devices, per_device(): lax.all_to_all(grad_coeff, 'dp', split_axis=1, concat_axis=0, tiled=True)  3.33 us
  transfers between devices with their start and end apart: 3, of which 2 were waited for; matrix products, arithmetic and copies ran while one was open for 11% of the time, Pallas kernels for 0%

commit v1 on v0

v1 whole, which is shorter than its diff:
```python
import jax
import jax.numpy as jnp
from jax import lax
from jax.sharding import PartitionSpec as P


def per_device(
    logits,
    token_ids,
    response_mask,
    lengths,
    prompt_of,
    old_logprob,
    ref_logprob,
    advantages,
    returns,
    critic_hidden,
    value_weight,
):
    seq_rows, seq_len, vocab_width = logits.shape
    all_seqs, tile_len, feat_count = critic_hidden.shape
    dp_size = lax.axis_size("dp")
    tensor_size = lax.axis_size("tensor")

    tile_rows = critic_hidden.reshape(all_seqs * tile_len, feat_count)
    tile_part = jnp.dot(tile_rows, value_weight, preferred_element_type=jnp.float32).reshape(
        all_seqs, tile_len
    )

    position = lax.broadcasted_iota(jnp.int32, (seq_rows, seq_len), 1)
    live_mask = (response_mask * (position < lengths[:, None]).astype(jnp.int32)).astype(
        jnp.float32
    )
    moments = jnp.stack(
        [
            jnp.sum(live_mask, axis=1),
            jnp.sum(live_mask * advantages, axis=1),
            jnp.sum(live_mask * advantages * advantages, axis=1),
            prompt_of.astype(jnp.float32),
        ],
        axis=1,
    )

    def by_tile(rows):
        return rows.reshape(seq_rows, dp_size, tile_len).transpose(1, 0, 2)

    def by_group(tile):
        return tile.reshape(dp_size, seq_rows, tile_len)

    block = jnp.concatenate(
        [
            by_group(tile_part),
            by_group(ref_logprob.astype(jnp.float32)),
            by_tile(returns),
            by_tile(live_mask),
            jnp.broadcast_to(moments[None], (dp_size, seq_rows, 4)),
        ],
        axis=2,
    )
    width = block.shape[2]
    send = jnp.broadcast_to(block[:, None], (dp_size, tensor_size, seq_rows, width)).reshape(
        dp_size * tensor_size, seq_rows, width
    )
    received = lax.all_to_all(send, ("dp", "tensor"), 0, 0, tiled=True).reshape(
        dp_size, tensor_size, seq_rows, width
    )

    local_top = jnp.max(logits, axis=2).astype(jnp.float32)
    vocab_start = lax.axis_index("tensor") * vocab_width
    shifted = token_ids - vocab_start
    column = lax.broadcasted_iota(jnp.int32, logits.shape, 2)
    wide = logits.astype(jnp.float32)
    local_sum = jnp.sum(jnp.exp(wide - local_top[:, :, None]), axis=2)
    local_target = jnp.sum(jnp.where(column == shifted[:, :, None], wide, 0.0), axis=2)

    shard_stats = lax.all_gather(
        jnp.stack(
            [local_top, local_sum, local_target, tile_part.reshape(seq_rows, seq_len)]
        ),
        "tensor",
    )
    tops = shard_stats[:, 0]
    row_max = jnp.max(tops, axis=0)
    total_sum = jnp.sum(shard_stats[:, 1] * jnp.exp(tops - row_max[None]), axis=0)
    target_logit = jnp.sum(shard_stats[:, 2], axis=0)
    tile_value = jnp.sum(shard_stats[:, 3], axis=0).reshape(all_seqs, tile_len)
    logprob = target_logit - (row_max + jnp.log(total_sum))

    def to_rows(blocks):
        return blocks.transpose(1, 0, 2).reshape(seq_rows, seq_len)

    first = received[:, 0]
    value_pred = to_rows(jnp.sum(received[:, :, :, :tile_len], axis=1))
    ref_rows = to_rows(first[:, :, tile_len : 2 * tile_len])
    tile_returns = first[:, :, 2 * tile_len : 3 * tile_len].reshape(all_seqs, tile_len)
    tile_mask = first[:, :, 3 * tile_len : 4 * tile_len].reshape(all_seqs, tile_len)
    seq_moments = first[:, :, 4 * tile_len :].reshape(all_seqs, 4)

    same = (prompt_of.astype(jnp.float32)[:, None] == seq_moments[None, :, 3]).astype(jnp.float32)
    count = jnp.sum(same * seq_moments[None, :, 0], axis=1)
    total = jnp.sum(same * seq_moments[None, :, 1], axis=1)
    square = jnp.sum(same * seq_moments[None, :, 2], axis=1)
    count_floor = jnp.maximum(count, 1.0)
    prompt_mean = total / count_floor
    prompt_var = (square - prompt_mean * total) / count_floor
    row_scale = lax.rsqrt(prompt_var + 1.0)
    whitened = (advantages - prompt_mean[:, None]) * row_scale[:, None]

    prob_ratio = jnp.exp(jnp.clip(logprob - old_logprob, -20.0, 20.0))
    surrogate = jnp.maximum(-whitened * prob_ratio, -whitened * jnp.clip(prob_ratio, 0.8, 1.2))
    surrogate = jnp.where(whitened < 0.0, jnp.minimum(surrogate, -3.0 * whitened), surrogate)
    ref_drift = jnp.clip(ref_rows - logprob, -20.0, 20.0)
    penalty = jnp.clip(jnp.exp(ref_drift) - ref_drift - 1.0, -10.0, 10.0)
    value_error = value_pred - returns
    token_loss = live_mask * (surrogate + 0.1 * penalty + 0.25 * value_error * value_error)

    head_weight = value_weight.astype(jnp.float32)
    grad_coeff = 32.0 * tile_mask * (tile_value - tile_returns)
    critic_grad = (grad_coeff[:, :, None] * head_weight[None, None, :]).astype(jnp.bfloat16)
    return (token_loss, critic_grad)


def solution(mesh):
    in_specs = (
        P("dp", None, "tensor"),
        P("dp", None),
        P("dp", None),
        P("dp"),
        P("dp"),
        P("dp", None),
        P(None, "dp"),
        P("dp", None),
        P("dp", None),
        P(None, "dp", "tensor"),
        P("tensor"),
    )
    out_specs = (P("dp", None), P(None, "dp", "tensor"))
    return jax.shard_map(
        per_device, mesh=mesh, in_specs=in_specs, out_specs=out_specs, check_vma=False
    )
```

time: 71.9 us -> 25.9 us (0.36)
  blocking collectives: 30 us -> 5.21 us
  waiting for transfers between devices: 12.2 us -> 0.01 us
  starting transfers between devices: 16 us -> 7.33 us
  matrix products: 2.1 us -> 0.24 us
  other arithmetic: 6.42 us -> 8.08 us
    psum x2 -> x0, blocking collectives: 23.4 us -> none  [the longest x1 17.7 us: per_device(): lax.psum((moments[0], moments[1], moments[2]), 'dp')]
    all_to_all x3 -> x1, waiting for transfers between devices: 12.2 us -> 0.01 us  [per_device(): lax.all_to_all(send, ('dp', 'tensor'), 0, 0, tiled=True)]
    all_to_all x3 -> x1, starting transfers between devices: 16 us -> 7.33 us  [per_device(): lax.all_to_all(send, ('dp', 'tensor'), 0, 0, tiled=True)]
    pmax x1 -> x0, blocking collectives: 6.63 us -> none  [per_device(): row_max = lax.pmax(local_top, 'tensor')]
    all_gather x0 -> x1, blocking collectives: none -> 5.21 us  [per_device(): lax.all_gather(jnp.stack([local_top, local_sum, local_target, tile_part.r...]
    gather x1 -> x0, local copies, waits for them, and re-layouts: 2.81 us -> none  [per_device(): jnp.take_along_axis(logits, clipped_ids[:, :, None], axis=2)[:, :, 0]]
    reduce_sum x2 -> x6, other arithmetic: 1.1 us -> 3.38 us  [the longest x1 2.07 us: per_device(): local_sum = jnp.sum(jnp.exp(wide - local_top[:, :, None]), axis=2)]
    all_to_all x1 -> x0, other arithmetic: 1.44 us -> none  [per_device(): lax.all_to_all(ref_logprob.astype(jnp.float32), 'dp', split_axis=0, conca...]
  transfers between devices with their start and end apart: 3 -> 1, of which waited for: 2 -> 0; matrix products, arithmetic and copies ran while one was open for 11% -> 17% of each run, Pallas kernels for 0% -> 0%
where the time goes in v1:
time: 25.9 us; the launch traced here: 25.6 us
  other arithmetic  8.08 us (31%)
  starting transfers between devices  7.33 us (28%)
  blocking collectives  5.21 us (20%)
  local copies, waits for them, and re-layouts  3.83 us (15%)
  between operations  0.86 us (3%)
    all_to_all x1, starting transfers between devices, per_device(): lax.all_to_all(send, ('dp', 'tensor'), 0, 0, tiled=True)  7.33 us
    all_gather x1, blocking collectives, per_device(): lax.all_gather(jnp.stack([local_top, local_sum, local_target, tile_part.r...  5.21 us
    reduce_max x1, other arithmetic, per_device(): local_top = jnp.max(logits, axis=2).astype(jnp.float32)  2.14 us
    reduce_sum x1, other arithmetic, per_device(): local_sum = jnp.sum(jnp.exp(wide - local_top[:, :, None]), axis=2)  2.07 us
    reduce_sum x1, other arithmetic, per_device(): jnp.sum(live_mask * advantages, axis=1)  1.04 us
    convert_element_type x1, other arithmetic, per_device(): (grad_coeff[:, :, None] * head_weight[None, None, :]).astype(jnp.bfloat16)  0.97 us
    reshape x2, local copies, waits for them, and re-layouts, by_tile(): return rows.reshape(seq_rows, dp_size, tile_len).transpose(1, 0, 2)  0.84 us
    convert_element_type x1, other arithmetic, per_device(): prompt_of.astype(jnp.float32)[:, None] == seq_moments[None, :, 3]  0.81 us
  transfers between devices with their start and end apart: 1, of which 0 were waited for; matrix products, arithmetic and copies ran while one was open for 17% of the time, Pallas kernels for 0%

profile of v1, /device:TPU:0, one launch (start us, length us, event | category | flops | bytes accessed | tf_op | source)
XLA Modules:
  0.0 25.6 jit_solution(2825822527815484801)
XLA Ops:
  0.6 0.0 copy-start
  0.7 0.8 %fusion.18 = (f32[2]{0:T(128)S(1)}, f32[2,1]{0,1:T(1,128)S(1)}) fusion(s32[2]{0:T(128)} %param.15), kind=kLoop, calls=%fused_computation.53 | loop fusion | flops 2 | bytes 24 | tf_op jit(solution)/shard_map/convert_element_type | solution.py:99
  1.5 1.0 %multiply_reduce_fusion.1 = (f32[2]{0:T(128)S(1)}, f32[2]{0:T(128)S(1)}, f32[2]{0:T(128)S(1)}, f32[2,128]{1,0:T(2,128)S(1)}) fusion(f32[2,128]{1,0:T(2,128)} %param.18, s32[2,128]{1,0:T(2,128)} %param.13, s32[2]{0:T(128)} %param.14), kind=kLoop, calls=%fused_computation.45 | loop fusion | flops 2042 | bytes 3104 | tf_op jit(solution)/shard_map/reduce_sum | solution.py:37
  2.5 0.1 copy.40
  2.6 0.7 %reshape.114 = bf16[1280,1]{0,1:T(2,128)(2,1)S(1)} reshape(bf16[1280]{0:T(1024)(128)(2,1)} %param.21) | data formatting | bytes 5120 | tf_op args[10]
  3.3 0.2 fusion.19
  3.6 0.2 reshape_reshape.3
  3.7 0.1 reshape.102
  3.8 0.8 %reshape.101 = f32[2,8,16]{2,1,0:T(8,128)S(1)} reshape(f32[2,128]{1,0:T(2,128)} %param.19) | data formatting | bytes 2048 | tf_op jit(solution)/shard_map/reshape | solution.py:45
  4.6 0.8 %concatenate.3 = f32[8,2,68]{2,1,0:T(2,128)S(1)} concatenate(f32[8,2,16]{2,1,0:T(2,128)S(1)} %reshape_reshape.3, bf16[8,2,16]{2,1,0:T(2,128)(2,1)} %bitcast.62, f32[8,2,16]{2,1,0:T(2,128)S(1)} %get-tuple-element.27, f32[8,2,16]{2,1,0:T(2,128)S(1)} %get-tuple-element.26, f32[8,2,4]{2,1,0:T(2,128)S(1)} %broadcast_in_dim.10), dimensions={2} | concatenate | bytes 8192 | tf_op jit(solution)/shard_map/concatenate | solution.py:50
  5.4 0.6 %broadcast_in_dim.11 = f32[8,4,2,68]{3,2,1,0:T(2,128)} broadcast(f32[8,2,68]{2,1,0:T(2,128)S(1)} %concatenate.3), dimensions={0,2,3} | broadcast | bytes 21760 | tf_op jit(solution)/shard_map/broadcast_in_dim | solution.py:61
  6.1 7.3 %all-to-all-start = ((f32[32,2,68]{2,1,0:T(2,128)}), f32[32,2,68]{2,1,0:T(2,128)S(1)}, u32[]{:S(2)}, u32[]{:S(2)}) async-start(f32[32,2,68]{2,1,0:T(2,128)} %bitcast.9), calls=%async_computation | async-start | bytes 65536 | tf_op jit(solution)/shard_map/all_to_all | solution.py:64
  13.4 2.1 %reduce_max.18 = bf16[2,128]{1,0:T(2,128)(2,1)S(1)} reduce(bf16[2,128,4864]{2,1,0:T(8,128)(2,1)} %param.11, bf16[]{:T(256)} %constant.9.clone.1), dimensions={2}, to_apply=%region_6.7 | reduce | flops 1244928 | bytes 2490882 | tf_op jit(solution)/shard_map/reduce_max | solution.py:68
  15.6 2.1 %fusion.1 = (f32[2,128]{1,0:T(2,128)S(1)}, f32[2,128]{1,0:T(2,128)S(1)}) fusion(bf16[2,128,4864]{2,1,0:T(8,128)(2,1)S(1)} %copy-done.1, f32[2,128]{1,0:T(2,128)S(1)} %get-tuple-element.25, s32[2,128]{1,0:T(2,128)S(1)} %broadcast_subtract_fusion), kind=kLoop, calls=%fused_computation.3 | loop fusion | flops 7470592 | bytes 2494464 | tf_op jit(solution)/shard_map/reduce_sum | solution.py:73
  17.7 5.2 %all-gather = f32[16,2,128]{2,1,0:T(2,128)S(1)} all-gather(f32[4,2,128]{2,1,0:T(2,128)S(1)} %pad_maximum_fusion), channel_id=2, replica_groups=mesh['dp'=8,'tensor'=4] {'tensor'}, dimensions={0}, use_global_device_ids=true | all-gather | bytes 20480 | tf_op jit(solution)/shard_map/all_gather | solution.py:76
  23.0 0.1 reshape.108
  23.1 0.1 slice.57
  23.2 0.1 fusion.17
  23.3 0.1 reshape.107
  23.3 0.2 slice_reduce_fusion.2
  23.6 0.1 reshape.106
  23.7 1.0 %multiply_convert_fusion = bf16[16,16,1280]{2,1,0:T(8,128)(2,1)} fusion(f32[1280]{0:T(1024)S(1)} %convert_element_type.44, f32[16,16]{1,0:T(8,128)S(1)} %subtract_multiply_fusion), kind=kLoop, calls=%fused_computation.6 | loop fusion | flops 655360 | bytes 661504 | tf_op jit(solution)/shard_map/convert_element_type | solution.py:119
  24.6 0.2 fusion.13
  24.9 0.6 %fusion.15 = f32[2,128]{1,0:T(2,128)} fusion(f32[2,128]{1,0:T(2,128)S(1)} %get-tuple-element.18, f32[2,128]{1,0:T(2,128)S(1)} %reshape.107, f32[2,128]{1,0:T(2,128)S(1)} %copy-done.4, f32[2,128]{1,0:T(2,128)S(1)} %reshape.106, f32[2,128]{1,0:T(2,128)S(1)} %copy-done.6, f32[2,128]{1,0:T(2,128)S(1)} %get-tuple-element.5, f32[2,128]{1,0:T(2,128)S(1)} %bitcast_reduce_fusion, ...), kind=kLoop, calls=%fused_computation.44 | loop fusion | flops 6912 | bytes 10256 | tf_op jit(solution)/shard_map/mul | solution.py:115
  (32 shorter events, 0.2 us)
Async XLA Ops:
  0.6 2.7 %copy-start = (bf16[16,16,1280]{2,1,0:T(8,128)(2,1)S(1)}, bf16[16,16,1280]{2,1,0:T(8,128)(2,1)}, u32[]{:S(2)}) copy-start(bf16[16,16,1280]{2,1,0:T(8,128)(2,1)} %param.20) | copy-start | bytes 1966084
  0.6 15.0 %copy-start.1 = (bf16[2,128,4864]{2,1,0:T(8,128)(2,1)S(1)}, bf16[2,128,4864]{2,1,0:T(8,128)(2,1)}, u32[]{:S(2)}) copy-start(bf16[2,128,4864]{2,1,0:T(8,128)(2,1)} %param.11) | copy-start | bytes 7471108
  0.7 14.9 %copy-start.5 = (s32[2,128]{1,0:T(2,128)S(1)}, s32[2,128]{1,0:T(2,128)}, u32[]{:S(2)}) copy-start(s32[2,128]{1,0:T(2,128)} %param.12) | copy-start | bytes 3076
  6.1 17.0 %all-to-all-start = ((f32[32,2,68]{2,1,0:T(2,128)}), f32[32,2,68]{2,1,0:T(2,128)S(1)}, u32[]{:S(2)}, u32[]{:S(2)}) async-start(f32[32,2,68]{2,1,0:T(2,128)} %bitcast.9), calls=%async_computation | async-start | bytes 65536 | tf_op jit(solution)/shard_map/all_to_all | solution.py:64
  13.4 9.6 %copy-start.2 = (bf16[1280]{0:T(1024)(128)(2,1)S(1)}, bf16[1280]{0:T(1024)(128)(2,1)}, u32[]{:S(2)}) copy-start(bf16[1280]{0:T(1024)(128)(2,1)} %param.21) | copy-start | bytes 7684
  13.4 11.5 %copy-start.3 = (f32[2,128]{1,0:T(2,128)S(1)}, f32[2,128]{1,0:T(2,128)}, u32[]{:S(2)}) copy-start(f32[2,128]{1,0:T(2,128)} %param.18) | copy-start | bytes 3076
  13.4 11.5 %copy-start.4 = (f32[2,128]{1,0:T(2,128)S(1)}, f32[2,128]{1,0:T(2,128)}, u32[]{:S(2)}) copy-start(f32[2,128]{1,0:T(2,128)} %param.19) | copy-start | bytes 3076
  13.4 11.5 %copy-start.6 = (f32[2,128]{1,0:T(2,128)S(1)}, f32[2,128]{1,0:T(2,128)}, u32[]{:S(2)}) copy-start(f32[2,128]{1,0:T(2,128)} %param.16) | copy-start | bytes 3076

commit v2 on v0

v2 whole, which is shorter than its diff:
```python
import functools

import jax
import jax.numpy as jnp
from jax import lax
from jax.experimental import pallas as pl
from jax.experimental.pallas import tpu as pltpu
from jax.sharding import PartitionSpec as P

LANES = 128
F32 = jnp.float32


def fold(x, period):
    shift = LANES // 2
    while shift >= period:
        x = x + pltpu.roll(x, shift, 1)
        shift //= 2
    return x


def in_hbm(*arrays):
    return [pltpu.with_memory_space_constraint(x, pltpu.HBM) for x in arrays]


def live_row(rmask_ref, len_ref, s):
    position = lax.broadcasted_iota(jnp.int32, (1, LANES), 1)
    return jnp.where(position < len_ref[s], rmask_ref[s : s + 1, :], 0).astype(F32)


def pre_kernel(
    dims, len_hbm, prompt_hbm, critic_hbm, w_hbm, refl_hbm, ret_hbm, rmask_hbm, adv_hbm,
    send_hbm, part_ref,
    len_ref, prompt_ref, critic_ref, w_ref, reflp_ref, ret_ref, rmask_ref, adv_ref, send_ref,
    wide_ref, sems,
):
    dp, tn, rows, tl = dims
    feat = critic_ref.shape[1]
    pairs = (
        (w_hbm, w_ref), (critic_hbm, critic_ref), (rmask_hbm, rmask_ref), (adv_hbm, adv_ref),
        (ret_hbm, ret_ref), (refl_hbm, reflp_ref), (len_hbm, len_ref), (prompt_hbm, prompt_ref),
    )
    copies = [pltpu.make_async_copy(a, b, sems.at[k]) for k, (a, b) in enumerate(pairs)]
    for copy in copies:
        copy.start()
    for copy in copies[2:]:
        copy.wait()
    wide_ref[:, 0:tl] = reflp_ref[...].astype(F32)
    sub = lax.broadcasted_iota(jnp.int32, (dp, LANES), 0)
    lane = lax.broadcasted_iota(jnp.int32, (dp, LANES), 1)
    slot = lane // tl
    blocks = []
    for s in range(rows):
        live = live_row(rmask_ref, len_ref, s)
        adv = adv_ref[s : s + 1, :]
        gain = live * adv
        refs = jnp.where(slot == 0, wide_ref[pl.ds(s, dp, stride=rows), :], 0.0)
        rets = jnp.where(slot == sub, jnp.broadcast_to(ret_ref[s : s + 1, :], (dp, LANES)), 0.0)
        lives = jnp.where(slot == sub, jnp.broadcast_to(live, (dp, LANES)), 0.0)
        block = jnp.where(slot == 1, fold(refs, tl), 0.0)
        block = jnp.where(slot == 2, fold(rets, tl), block)
        block = jnp.where(slot == 3, fold(lives, tl), block)
        block = jnp.where(lane == 4 * tl, jnp.sum(live, axis=1, keepdims=True), block)
        block = jnp.where(lane == 4 * tl + 1, jnp.sum(gain, axis=1, keepdims=True), block)
        block = jnp.where(lane == 4 * tl + 2, jnp.sum(gain * adv, axis=1, keepdims=True), block)
        block = jnp.where(lane == 4 * tl + 3, prompt_ref[s].astype(F32), block)
        blocks.append(block)
    for copy in copies[:2]:
        copy.wait()
    weights = jnp.broadcast_to(w_ref[...][None, :], (16, feat))
    flat = lax.dot_general(
        weights, critic_ref[...], (((1,), (1,)), ((), ())), preferred_element_type=F32
    )
    for h in range(rows):
        part_ref[h : h + 1, :] = flat[0:1, h * LANES : (h + 1) * LANES]
    for s in range(rows):
        value = jnp.zeros((dp, LANES), F32)
        for h in range(rows):
            line = jnp.broadcast_to(flat[0:1, h * LANES : (h + 1) * LANES], (dp, LANES))
            value = jnp.where((h * LANES + lane) // tl == sub * rows + s, line, value)
        block = jnp.where(slot == 0, fold(value, tl), blocks[s])
        for j in range(tn):
            send_ref[pl.ds(j * rows + s, dp, stride=tn * rows), :] = block
    out = pltpu.make_async_copy(send_ref, send_hbm, sems.at[len(pairs)])
    out.start()
    out.wait()


def stats_kernel(
    ids_hbm, part_ref, logits_hbm, out_ref,
    logits_ref, ids_ref, id_ref, top_ref, sum_ref, hit_ref, sems, ids_sem,
):
    rows, tokens, width = logits_ref.shape
    steps = sems.shape[1]
    step = tokens // steps
    copies = [
        [
            pltpu.make_async_copy(
                logits_hbm.at[s, pl.ds(k * step, step)],
                logits_ref.at[s, pl.ds(k * step, step)],
                sems.at[s, k],
            )
            for k in range(steps)
        ]
        for s in range(rows)
    ]
    ids_copy = pltpu.make_async_copy(ids_hbm, ids_ref, ids_sem)
    ids_copy.start()
    for row in copies:
        for copy in row:
            copy.start()
    start = lax.axis_index("tensor") * width
    lane = lax.broadcasted_iota(jnp.int32, (tokens, LANES), 1)
    ids_copy.wait()
    for s in range(rows):
        ids = jnp.broadcast_to(ids_ref[s : s + 1, :].astype(F32), (LANES, tokens))
        shifted = jnp.transpose(ids).astype(jnp.int32) - start
        id_ref[s] = jnp.where(lane == (shifted & (LANES - 1)), shifted >> 7, -1)
    for s in range(rows):
        for k in range(steps):
            copies[s][k].wait()
            at = slice(k * step, (k + 1) * step)
            top = logits_ref[s, at, 0:LANES]
            for c in range(1, width // LANES):
                top = jnp.maximum(top, logits_ref[s, at, c * LANES : (c + 1) * LANES])
            top = jnp.max(top.astype(F32), axis=1, keepdims=True)
            hot = id_ref[s, at, :]
            total = jnp.zeros((step, LANES), F32)
            hit = jnp.zeros((step, LANES), F32)
            for c in range(width // LANES):
                x = logits_ref[s, at, c * LANES : (c + 1) * LANES].astype(F32)
                total = total + jnp.exp(x - top)
                hit = jnp.where(hot == c, x, hit)
            top_ref[at, :] = jnp.broadcast_to(top, (step, LANES))
            sum_ref[at, :] = total
            hit_ref[at, :] = hit
        out_ref[s : s + 1, :] = jnp.transpose(top_ref[...])[0:1, :]
        out_ref[rows + s : rows + s + 1, :] = jnp.sum(
            jnp.transpose(sum_ref[...]), axis=0, keepdims=True
        )
        out_ref[2 * rows + s : 2 * rows + s + 1, :] = jnp.sum(
            jnp.transpose(hit_ref[...]), axis=0, keepdims=True
        )
    out_ref[3 * rows : 4 * rows, :] = part_ref[...]


def post_kernel(
    dims, len_ref, prompt_ref, recv_ref, stats_ref, w_ref, old_ref, adv_ref, ret_ref, rmask_ref,
    loss_ref, grad_ref,
):
    dp, tn, rows, tl = dims
    seqs = dp * rows
    sub = lax.broadcasted_iota(jnp.int32, (dp, LANES), 0)
    lane = lax.broadcasted_iota(jnp.int32, (dp, LANES), 1)
    slot = lane // tl

    def pick(x, k):
        return fold(jnp.where(slot == k, x, 0.0), tl)

    def down(x):
        return jnp.sum(x, axis=0, keepdims=True)

    firsts, values, refs = [], [], []
    flat_ret = [jnp.zeros((1, LANES), F32) for _ in range(rows)]
    flat_live = [jnp.zeros((1, LANES), F32) for _ in range(rows)]
    for s in range(rows):
        parts = [recv_ref[pl.ds(j * rows + s, dp, stride=tn * rows), :] for j in range(tn)]
        first = parts[0]
        every = sum(parts[1:], first)
        firsts.append(first)
        values.append(down(jnp.where(slot == sub, pick(every, 0), 0.0)))
        refs.append(down(jnp.where(slot == sub, pick(first, 1), 0.0)))
        tile_ret, tile_live = pick(first, 2), pick(first, 3)
        for h in range(rows):
            here = (h * LANES + lane) // tl == sub * rows + s
            flat_ret[h] += down(jnp.where(here, tile_ret, 0.0))
            flat_live[h] += down(jnp.where(here, tile_live, 0.0))

    seq_sub = lax.broadcasted_iota(jnp.int32, (seqs, LANES), 0)
    seq_lane = lax.broadcasted_iota(jnp.int32, (seqs, LANES), 1)
    coeff = jnp.zeros((seqs, LANES), F32)
    for h in range(rows):
        tile_value = stats_ref[0, 3 * rows + h : 3 * rows + h + 1, :]
        for j in range(1, tn):
            tile_value += stats_ref[j, 3 * rows + h : 3 * rows + h + 1, :]
        line = 32.0 * flat_live[h] * (tile_value - flat_ret[h])
        here = (h * LANES + seq_lane) // tl == seq_sub
        coeff = jnp.where(here, jnp.broadcast_to(line, (seqs, LANES)), coeff)
    columns = jnp.transpose(fold(coeff, tl))
    weights = w_ref[...].astype(F32)
    for b in range(seqs):
        grad_ref[b] = (columns[0:tl, b : b + 1] * weights).astype(grad_ref.dtype)

    for s in range(rows):
        live = live_row(rmask_ref, len_ref, s)
        own = prompt_ref[s].astype(F32)
        sums = jnp.zeros((1, LANES), F32)
        for first in firsts:
            sums += down(jnp.where(first[:, 4 * tl + 3 : 4 * tl + 4] == own, first, 0.0))
        count = jnp.maximum(sums[:, 4 * tl : 4 * tl + 1], 1.0)
        total = sums[:, 4 * tl + 1 : 4 * tl + 2]
        mean = total / count
        var = (sums[:, 4 * tl + 2 : 4 * tl + 3] - mean * total) / count
        whitened = (adv_ref[s : s + 1, :] - mean) * lax.rsqrt(var + 1.0)

        tops = [stats_ref[j, s : s + 1, :] for j in range(tn)]
        row_max = functools.reduce(jnp.maximum, tops)
        exp_sum = sum(
            stats_ref[j, rows + s : rows + s + 1, :] * jnp.exp(tops[j] - row_max)
            for j in range(tn)
        )
        target = sum(stats_ref[j, 2 * rows + s : 2 * rows + s + 1, :] for j in range(tn))
        logprob = target - (row_max + jnp.log(exp_sum))

        ratio = jnp.exp(jnp.clip(logprob - old_ref[s : s + 1, :], -20.0, 20.0))
        surrogate = jnp.maximum(-whitened * ratio, -whitened * jnp.clip(ratio, 0.8, 1.2))
        surrogate = jnp.where(whitened < 0.0, jnp.minimum(surrogate, -3.0 * whitened), surrogate)
        drift = jnp.clip(refs[s] - logprob, -20.0, 20.0)
        penalty = jnp.clip(jnp.exp(drift) - drift - 1.0, -10.0, 10.0)
        error = values[s] - ret_ref[s : s + 1, :]
        loss_ref[s : s + 1, :] = live * (surrogate + 0.1 * penalty + 0.25 * error * error)


def per_device(
    logits,
    token_ids,
    response_mask,
    lengths,
    prompt_of,
    old_logprob,
    ref_logprob,
    advantages,
    returns,
    critic_hidden,
    value_weight,
):
    rows, tokens, width = logits.shape
    seqs, tl, feat = critic_hidden.shape
    dp, tn = lax.axis_size("dp"), lax.axis_size("tensor")
    dims = (dp, tn, rows, tl)
    if tokens != LANES or width % LANES or 5 * tl > LANES or LANES % tl or tl < 1:
        raise ValueError("unsupported shapes")
    smem = pl.BlockSpec(memory_space=pltpu.SMEM)
    vmem = pl.BlockSpec(memory_space=pltpu.VMEM)
    weight_row = value_weight[None, :]

    hbm = pl.BlockSpec(memory_space=pltpu.HBM)
    send, part = pl.pallas_call(
        functools.partial(pre_kernel, dims),
        name="pre",
        out_shape=(
            jax.ShapeDtypeStruct((dp * tn * rows, LANES), F32),
            jax.ShapeDtypeStruct((rows, LANES), F32),
        ),
        in_specs=[hbm] * 8,
        out_specs=(hbm, vmem),
        scratch_shapes=[
            pltpu.SMEM(lengths.shape, jnp.int32),
            pltpu.SMEM(prompt_of.shape, jnp.int32),
            pltpu.VMEM((seqs * tl, feat), jnp.bfloat16),
            pltpu.VMEM((feat,), jnp.bfloat16),
            pltpu.VMEM((seqs, tl), jnp.bfloat16),
            pltpu.VMEM((rows, LANES), F32),
            pltpu.VMEM((rows, LANES), jnp.int32),
            pltpu.VMEM((rows, LANES), F32),
            pltpu.VMEM((dp * tn * rows, LANES), F32),
            pltpu.VMEM((seqs, LANES), F32),
            pltpu.SemaphoreType.DMA((9,)),
        ],
        compiler_params=pltpu.CompilerParams(vmem_limit_bytes=6 << 20),
        cost_estimate=pl.CostEstimate(
            flops=40_000_000, bytes_accessed=8_000_000, transcendentals=0
        ),
    )(
        *in_hbm(
            lengths, prompt_of, critic_hidden.reshape(seqs * tl, feat), value_weight, ref_logprob,
            returns, response_mask, advantages,
        )
    )
    received = lax.all_to_all(
        send.reshape(dp * tn, rows, LANES), ("dp", "tensor"), 0, 0, tiled=True
    ).reshape(dp * tn * rows, LANES)

    stats = pl.pallas_call(
        stats_kernel,
        name="stats",
        out_shape=jax.ShapeDtypeStruct((4 * rows, LANES), F32),
        in_specs=[hbm, vmem, hbm],
        out_specs=vmem,
        scratch_shapes=[
            pltpu.VMEM(logits.shape, logits.dtype),
            pltpu.VMEM((rows, tokens), jnp.int32),
            pltpu.VMEM((rows, LANES, LANES), jnp.int32),
            pltpu.VMEM((LANES, LANES), F32),
            pltpu.VMEM((LANES, LANES), F32),
            pltpu.VMEM((LANES, LANES), F32),
            pltpu.SemaphoreType.DMA((rows, 4)),
            pltpu.SemaphoreType.DMA,
        ],
        compiler_params=pltpu.CompilerParams(vmem_limit_bytes=8 << 20),
        cost_estimate=pl.CostEstimate(
            flops=8 * logits.size, bytes_accessed=2 * logits.size, transcendentals=logits.size
        ),
    )(*in_hbm(token_ids), part, *in_hbm(logits))
    gathered = lax.all_gather(stats, "tensor")

    return pl.pallas_call(
        functools.partial(post_kernel, dims),
        name="post",
        compiler_params=pltpu.CompilerParams(vmem_limit_bytes=6 << 20),
        out_shape=(
            jax.ShapeDtypeStruct((rows, tokens), F32),
            jax.ShapeDtypeStruct((seqs, tl, feat), jnp.bfloat16),
        ),
        in_specs=[smem, smem] + [vmem] * 7,
        out_specs=(vmem, vmem),
    )(
        lengths, prompt_of, received, gathered, weight_row, old_logprob, advantages, returns,
        response_mask,
    )


def solution(mesh):
    in_specs = (
        P("dp", None, "tensor"),
        P("dp", None),
        P("dp", None),
        P("dp"),
        P("dp"),
        P("dp", None),
        P(None, "dp"),
        P("dp", None),
        P("dp", None),
        P(None, "dp", "tensor"),
        P("tensor"),
    )
    out_specs = (P("dp", None), P(None, "dp", "tensor"))
    return jax.shard_map(
        per_device, mesh=mesh, in_specs=in_specs, out_specs=out_specs, check_vma=False
    )
```

time: 71.9 us -> 22.3 us (0.31)
  blocking collectives: 30 us -> 5.21 us
  waiting for transfers between devices: 12.2 us -> 0.01 us
  starting transfers between devices: 16 us -> 7.33 us
  Pallas kernels: 0 us -> 8.09 us
  other arithmetic: 6.42 us -> 0 us
  local copies, waits for them, and re-layouts: 3.95 us -> 0.72 us
  matrix products: 2.1 us -> 0 us
    psum x2 -> x0, blocking collectives: 23.4 us -> none  [the longest x1 17.7 us: per_device(): lax.psum((moments[0], moments[1], moments[2]), 'dp')]
    all_to_all x3 -> x1, waiting for transfers between devices: 12.2 us -> 0.01 us  [per_device(): lax.all_to_all(send.reshape(dp * tn, rows, LANES), ('dp', 'tensor'), 0, 0...]
    all_to_all x3 -> x1, starting transfers between devices: 16 us -> 7.33 us  [per_device(): lax.all_to_all(send.reshape(dp * tn, rows, LANES), ('dp', 'tensor'), 0, 0...]
    pallas_call x0 -> x3, Pallas kernels: none -> 8.09 us  [the longest x1 3.45 us: per_device(): pl.pallas_call(stats_kernel, name='stats', out_shape=jax.ShapeDtypeStruct...]
    pmax x1 -> x0, blocking collectives: 6.63 us -> none  [per_device(): row_max = lax.pmax(local_top, 'tensor')]
    all_gather x0 -> x1, blocking collectives: none -> 5.21 us  [per_device(): gathered = lax.all_gather(stats, 'tensor')]
    gather x1 -> x0, local copies, waits for them, and re-layouts: 2.81 us -> none  [per_device(): jnp.take_along_axis(logits, clipped_ids[:, :, None], axis=2)[:, :, 0]]
    reduce_max x1 -> x0, other arithmetic: 2.13 us -> none  [per_device(): local_top = jnp.max(logits, axis=2).astype(jnp.float32)]
  transfers between devices with their start and end apart: 3 -> 1, of which waited for: 2 -> 0; matrix products, arithmetic and copies ran while one was open for 11% -> 3% of each run, Pallas kernels for 0% -> 16%
where the time goes in v2:
time: 22.3 us; the launch traced here: 22.1 us
  Pallas kernels  8.09 us (36%)
  starting transfers between devices  7.33 us (33%)
  blocking collectives  5.21 us (23%)
  between operations  0.73 us (3%)
  local copies, waits for them, and re-layouts  0.72 us (3%)
    all_to_all x1, starting transfers between devices, per_device(): lax.all_to_all(send.reshape(dp * tn, rows, LANES), ('dp', 'tensor'), 0, 0...  7.33 us
    all_gather x1, blocking collectives, per_device(): gathered = lax.all_gather(stats, 'tensor')  5.21 us
    pallas_call x1, Pallas kernels, per_device(): pl.pallas_call(stats_kernel, name='stats', out_shape=jax.ShapeDtypeStruct...  3.45 us
    pallas_call x1, Pallas kernels, per_device(): pl.pallas_call(functools.partial(pre_kernel, dims), name='pre', out_shape...  2.45 us
    pallas_call x1, Pallas kernels, per_device(): pl.pallas_call(functools.partial(post_kernel, dims), name='post', compile...  2.19 us
    broadcast_in_dim x1, local copies, waits for them, and re-layouts, per_device(): weight_row = value_weight[None, :]  0.69 us
  transfers between devices with their start and end apart: 1, of which 0 were waited for; matrix products, arithmetic and copies ran while one was open for 3% of the time, Pallas kernels for 16%

profile of v2, /device:TPU:0, one launch (start us, length us, event | category | flops | bytes accessed | tf_op | source)
XLA Modules:
  0.0 22.1 jit_solution(14242563785602357872)
XLA Ops:
  0.6 0.0 copy-start
  0.6 0.0 copy-start.2
  0.7 0.0 copy-start.4
  0.7 0.0 copy-start.3
  0.7 0.0 copy-start.1
  0.7 0.0 copy-start.5
  0.7 2.4 %pre.1 = (f32[64,128]{1,0:T(8,128)}, f32[2,128]{1,0:T(2,128)S(1)}) custom-call(s32[2]{0:T(128)} %len_ref.1, s32[2]{0:T(128)} %prompt_ref.1, bf16[256,1280]{1,0:T(8,128)(2,1)} %bitcast.6, bf16[1280]{0:T(1024)(128)(2,1)} %w_hbm.1, bf16[16,16]{1,0:T(8,128)(2,1)} %refl_hbm.1, f32[2,128]{1,0:T(2,128)} %ret_ref.1, s32[2,128]{1,0:T(2,128)} %rmask_ref.1, ...), custom_call_target="tpu_custom_call" | custom-call | flops 40000000 | bytes 8000000 | tf_op jit(solution)/shard_map/pre/pallas_call | solution.py:248
  3.1 7.3 %all-to-all-start = ((f32[32,2,128]{2,1,0:T(2,128)}), f32[32,2,128]{2,1,0:T(2,128)S(1)}, u32[]{:S(2)}, u32[]{:S(2)}) async-start(f32[32,2,128]{2,1,0:T(2,128)} %bitcast.1), calls=%async_computation | async-start | bytes 65536 | tf_op jit(solution)/shard_map/all_to_all | solution.py:280
  10.5 0.7 %broadcast_in_dim.3.w_ref = bf16[1,1280]{1,0:T(2,128)(2,1)S(1)} reshape(bf16[1280]{0:T(1024)(128)(2,1)} %w_hbm.1) | data formatting | bytes 5120 | tf_op jit(solution)/shard_map/broadcast_in_dim | solution.py:245
  11.2 3.5 %stats.1 = f32[8,128]{1,0:T(8,128)S(1)} custom-call(s32[2,128]{1,0:T(2,128)} %ids_hbm.1, f32[2,128]{1,0:T(2,128)S(1)} %get-tuple-element.5.part_ref, bf16[2,128,4864]{2,1,0:T(8,128)(2,1)} %logits_hbm.1), custom_call_target="tpu_custom_call" | custom-call | flops 9961472 | bytes 2490368 | tf_op jit(solution)/shard_map/stats/pallas_call | solution.py:284
  14.6 5.2 %all-gather = f32[32,128]{1,0:T(8,128)S(1)} all-gather(f32[8,128]{1,0:T(8,128)S(1)} %stats.1), channel_id=2, replica_groups=mesh['dp'=8,'tensor'=4] {'tensor'}, dimensions={0}, use_global_device_ids=true | all-gather | bytes 20480 | tf_op jit(solution)/shard_map/all_gather | solution.py:305
  19.8 0.0 all-to-all-done
  19.8 0.0 copy-done
  19.9 0.0 copy-done.2
  19.9 0.0 copy-done.4
  19.9 0.0 copy-done.3
  19.9 0.0 copy-done.1
  19.9 0.0 copy-done.5
  19.9 2.2 %post.1 = (f32[2,128]{1,0:T(2,128)}, bf16[16,16,1280]{2,1,0:T(8,128)(2,1)}) custom-call(s32[2]{0:T(128)S(1)} %copy-done.3, s32[2]{0:T(128)S(1)} %copy-done.4, f32[64,128]{1,0:T(8,128)S(1)} %bitcast.4, f32[4,8,128]{2,1,0:T(8,128)S(1)} %bitcast.5, bf16[1,1280]{1,0:T(2,128)(2,1)S(1)} %broadcast_in_dim.3.w_ref, f32[2,128]{1,0:T(2,128)S(1)} %copy-done.5, ...), custom_call_target="tpu_custom_call" | custom-call | tf_op jit(solution)/shard_map/post/pallas_call | solution.py:307
Async XLA Ops:
  0.6 19.2 %copy-start = (f32[2,128]{1,0:T(2,128)S(1)}, f32[2,128]{1,0:T(2,128)}, u32[]{:S(2)}) copy-start(f32[2,128]{1,0:T(2,128)} %ret_ref.1) | copy-start | bytes 3076
  0.6 19.2 %copy-start.2 = (f32[2,128]{1,0:T(2,128)S(1)}, f32[2,128]{1,0:T(2,128)}, u32[]{:S(2)}) copy-start(f32[2,128]{1,0:T(2,128)} %adv_ref.1) | copy-start | bytes 3076
  0.7 19.2 %copy-start.4 = (s32[2]{0:T(128)S(1)}, s32[2]{0:T(128)}, u32[]{:S(2)}) copy-start(s32[2]{0:T(128)} %prompt_ref.1) | copy-start | bytes 28
  0.7 19.2 %copy-start.3 = (s32[2]{0:T(128)S(1)}, s32[2]{0:T(128)}, u32[]{:S(2)}) copy-start(s32[2]{0:T(128)} %len_ref.1) | copy-start | bytes 28
  0.7 19.2 %copy-start.1 = (s32[2,128]{1,0:T(2,128)S(1)}, s32[2,128]{1,0:T(2,128)}, u32[]{:S(2)}) copy-start(s32[2,128]{1,0:T(2,128)} %rmask_ref.1) | copy-start | bytes 3076
  0.7 19.2 %copy-start.5 = (f32[2,128]{1,0:T(2,128)S(1)}, f32[2,128]{1,0:T(2,128)}, u32[]{:S(2)}) copy-start(f32[2,128]{1,0:T(2,128)} %old_ref.1) | copy-start | bytes 3076
  3.1 16.7 %all-to-all-start = ((f32[32,2,128]{2,1,0:T(2,128)}), f32[32,2,128]{2,1,0:T(2,128)S(1)}, u32[]{:S(2)}, u32[]{:S(2)}) async-start(f32[32,2,128]{2,1,0:T(2,128)} %bitcast.1), calls=%async_computation | async-start | bytes 65536 | tf_op jit(solution)/shard_map/all_to_all | solution.py:280

commit v3 on v2

v3 whole, which is shorter than its diff:
```python
import functools

import jax
import jax.numpy as jnp
from jax import lax
from jax.experimental import pallas as pl
from jax.experimental.pallas import tpu as pltpu
from jax.sharding import PartitionSpec as P

LANES = 128
F32 = jnp.float32


def fold(x, period):
    shift = LANES // 2
    while shift >= period:
        x = x + pltpu.roll(x, shift, 1)
        shift //= 2
    return x


def in_hbm(*arrays):
    return [pltpu.with_memory_space_constraint(x, pltpu.HBM) for x in arrays]


def live_row(rmask_ref, len_ref, s):
    position = lax.broadcasted_iota(jnp.int32, (1, LANES), 1)
    return jnp.where(position < len_ref[s], rmask_ref[s : s + 1, :], 0).astype(F32)


def group_grid(dp, tl):
    group = lax.broadcasted_iota(jnp.int32, (dp, LANES), 0)
    lane = lax.broadcasted_iota(jnp.int32, (dp, LANES), 1)
    return group, lane, lane // tl


def is_early():
    return lax.axis_index("dp") == 0


def lane_sums(wide):
    total = wide[:, 0:LANES]
    whole = wide.shape[1] // LANES
    for c in range(1, whole):
        total = total + wide[:, c * LANES : (c + 1) * LANES]
    left = wide.shape[1] - whole * LANES
    if left:
        pad = jnp.zeros((wide.shape[0], LANES - left), F32)
        total = total + jnp.concatenate([wide[:, whole * LANES :], pad], axis=1)
    return total


def pre_kernel(
    dims, len_hbm, prompt_hbm, critic_hbm, w_hbm, refl_hbm, ret_hbm, rmask_hbm, adv_hbm,
    ids_hbm, logits_hbm,
    send_hbm, stats_ref,
    len_ref, prompt_ref, critic_ref, w_ref, reflp_ref, ret_ref, rmask_ref, adv_ref, send_ref,
    wide_ref, sems, *scratch,
):
    dp, tn, rows, tl = dims
    pairs = (
        (w_hbm, w_ref), (critic_hbm, critic_ref), (rmask_hbm, rmask_ref), (adv_hbm, adv_ref),
        (ret_hbm, ret_ref), (refl_hbm, reflp_ref), (len_hbm, len_ref), (prompt_hbm, prompt_ref),
    )
    copies = [pltpu.make_async_copy(a, b, sems.at[k]) for k, (a, b) in enumerate(pairs)]
    for copy in copies:
        copy.start()
    for copy in copies[2:]:
        copy.wait()
    wide_ref[:, 0:tl] = reflp_ref[...].astype(F32)
    group, lane, slot = group_grid(dp, tl)
    blocks = []
    for s in range(rows):
        live = live_row(rmask_ref, len_ref, s)
        adv = adv_ref[s : s + 1, :]
        gain = live * adv
        refs = pltpu.roll(wide_ref[pl.ds(s, dp, stride=rows), :], tl, 1)
        rets = jnp.where(slot == group, jnp.broadcast_to(ret_ref[s : s + 1, :], (dp, LANES)), 0.0)
        lives = jnp.where(slot == group, jnp.broadcast_to(live, (dp, LANES)), 0.0)
        block = jnp.where(slot == 1, refs, 0.0)
        block = jnp.where(slot == 2, fold(rets, tl), block)
        block = jnp.where(slot == 3, fold(lives, tl), block)
        block = jnp.where(lane == 4 * tl, jnp.sum(live, axis=1, keepdims=True), block)
        block = jnp.where(lane == 4 * tl + 1, jnp.sum(gain, axis=1, keepdims=True), block)
        block = jnp.where(lane == 4 * tl + 2, jnp.sum(gain * adv, axis=1, keepdims=True), block)
        block = jnp.where(lane == 4 * tl + 3, prompt_ref[s].astype(F32), block)
        blocks.append(block)
    for copy in copies[:2]:
        copy.wait()
    weights = w_ref[...][None, :].astype(F32)
    flat = []
    for h in range(rows):
        wide = critic_ref[h * LANES : (h + 1) * LANES, :].astype(F32) * weights
        flat.append(jnp.sum(jnp.transpose(lane_sums(wide)), axis=0, keepdims=True))
    for h in range(rows):
        stats_ref[3 * rows + h : 3 * rows + h + 1, :] = flat[h]
    for s in range(rows):
        value = jnp.zeros((dp, LANES), F32)
        for h in range(rows):
            line = jnp.broadcast_to(flat[h], (dp, LANES))
            value = jnp.where((h * LANES + lane) // tl == group * rows + s, line, value)
        block = jnp.where(slot == 0, fold(value, tl), blocks[s])
        for j in range(tn):
            send_ref[pl.ds(j * rows + s, dp, stride=tn * rows), :] = block
    out = pltpu.make_async_copy(send_ref, send_hbm, sems.at[len(pairs)])
    out.start()

    @pl.when(is_early())
    def _():
        run_stats(ids_hbm, logits_hbm, stats_ref, *scratch)

    out.wait()


def run_stats(
    ids_hbm, logits_hbm, out_ref,
    logits_ref, ids_ref, ids_smem, here_ref, top_ref, sum_ref, hit_ref, sems, ids_sems,
):
    rows, tokens, width = logits_ref.shape
    chunks = width // LANES
    steps = sems.shape[1]
    step = tokens // steps
    blocks = [(s, k) for s in range(rows) for k in range(steps)]
    copies = [
        pltpu.make_async_copy(
            logits_hbm.at[s, pl.ds(k * step, step)],
            logits_ref.at[s, pl.ds(k * step, step)],
            sems.at[s, k],
        )
        for s, k in blocks
    ]
    ids_copies = [
        pltpu.make_async_copy(ids_hbm, ids_ref, ids_sems.at[0]),
        pltpu.make_async_copy(ids_hbm, ids_smem, ids_sems.at[1]),
    ]
    for copy in ids_copies + copies:
        copy.start()
    start = lax.axis_index("tensor") * width
    lane = lax.broadcasted_iota(jnp.int32, (tokens, LANES), 1)
    for copy in ids_copies:
        copy.wait()
    for s in range(rows):
        ids = jnp.broadcast_to(ids_ref[s : s + 1, :].astype(F32), (LANES, tokens))
        shifted = jnp.transpose(ids).astype(jnp.int32) - start
        here = (lane == (shifted & (LANES - 1))) & (shifted >= 0) & (shifted < width)
        here_ref[s] = here.astype(F32)

    def part_of(n, c):
        s, k = blocks[n]
        return logits_ref[s, k * step : (k + 1) * step, c * LANES : (c + 1) * LANES]

    def shift_of(n):
        copies[n].wait()
        return jnp.max(part_of(n, 0).astype(F32), axis=1, keepdims=True)

    over_lanes = (((1,), (1,)), ((), ()))
    ones = jnp.ones((16, LANES), jnp.bfloat16)

    def sum_row(s):
        return jnp.sum(jnp.transpose(sum_ref[s]), axis=0, keepdims=True)

    def top_row(s):
        return lax.dot_general(
            ones * (1.0 / LANES), top_ref[s], over_lanes, preferred_element_type=F32
        )[0:1, :]

    row8 = lax.broadcasted_iota(jnp.int32, (8, LANES), 0)
    worst = jnp.zeros((8, LANES), F32)
    top = shift_of(0)
    for n, (s, k) in enumerate(blocks):
        later = shift_of(n + 1) if n + 1 < len(blocks) else None
        at = slice(k * step, (k + 1) * step)
        total = jnp.zeros((step, LANES), F32)
        for c in range(chunks):
            total = total + jnp.exp(part_of(n, c).astype(F32) - top)
        top_ref[s, at, :] = jnp.broadcast_to(top, (step, LANES)).astype(jnp.bfloat16)
        sum_ref[s, at, :] = total
        for q in range(step // 8):
            worst = jnp.maximum(worst, total[q * 8 : (q + 1) * 8, :])
            first = k * step + q * 8
            hit = jnp.zeros((8, LANES), F32)
            for r in range(8):
                chunk = jnp.clip((ids_smem[s, first + r] - start) >> 7, 0, chunks - 1)
                cols = pl.ds(pl.multiple_of(chunk * LANES, LANES), LANES)
                x = logits_ref[s, first : first + 8, cols].astype(F32)
                hit = jnp.where(row8 == r, x, hit)
            here = here_ref[s, first : first + 8, :] > 0.0
            hit_ref[s, first : first + 8, :] = jnp.where(here, hit, 0.0)
        top = later
        if k == steps - 1:
            hits = lax.dot_general(
                ones, hit_ref[s].astype(jnp.bfloat16), over_lanes, preferred_element_type=F32
            )
            out_ref[s : s + 1, :] = top_row(s)
            out_ref[rows + s : rows + s + 1, :] = sum_row(s)
            out_ref[2 * rows + s : 2 * rows + s + 1, :] = hits[0:1, :]

    @pl.when(jnp.logical_not(jnp.max(worst) < 1e30))
    def _():
        for s in range(rows):

            def again(k, carry, s=s):
                at = pl.ds(pl.multiple_of(k * 32, 32), 32)
                top = logits_ref[s, at, 0:LANES]
                for c in range(1, chunks):
                    top = jnp.maximum(top, logits_ref[s, at, c * LANES : (c + 1) * LANES])
                top = jnp.max(top.astype(F32), axis=1, keepdims=True)
                total = jnp.zeros((32, LANES), F32)
                for c in range(chunks):
                    x = logits_ref[s, at, c * LANES : (c + 1) * LANES].astype(F32)
                    total = total + jnp.exp(x - top)
                top_ref[s, at, :] = jnp.broadcast_to(top, (32, LANES)).astype(jnp.bfloat16)
                sum_ref[s, at, :] = total
                return carry

            lax.fori_loop(0, tokens // 32, again, 0)
            out_ref[s : s + 1, :] = top_row(s)
            out_ref[rows + s : rows + s + 1, :] = sum_row(s)


def stats_kernel(ids_hbm, early_ref, logits_hbm, out_ref, *scratch):
    out_ref[...] = early_ref[...]

    @pl.when(jnp.logical_not(is_early()))
    def _():
        run_stats(ids_hbm, logits_hbm, out_ref, *scratch)


def merge_kernel(dims, old_ref, *refs):
    dp, tn, rows, tl = dims
    stats, (logprob_ref, ratio_ref, tile_ref) = refs[:tn], refs[tn:]
    seqs = dp * rows
    tops = [stat[0:rows, :] for stat in stats]
    row_max = functools.reduce(jnp.maximum, tops)
    exp_sum = sum(
        stat[rows : 2 * rows, :] * jnp.exp(top - row_max) for stat, top in zip(stats, tops)
    )
    target = sum(stat[2 * rows : 3 * rows, :] for stat in stats)
    logprob = target - (row_max + jnp.log(exp_sum))
    logprob_ref[...] = logprob
    ratio_ref[...] = jnp.exp(jnp.clip(logprob - old_ref[...], -20.0, 20.0))

    order = lax.broadcasted_iota(jnp.int32, (seqs, LANES), 0)
    seq = (order % dp) * rows + order // dp
    lane = lax.broadcasted_iota(jnp.int32, (seqs, LANES), 1)
    tile = jnp.zeros((seqs, LANES), F32)
    for h in range(rows):
        line = sum(stat[3 * rows + h : 3 * rows + h + 1, :] for stat in stats)
        here = (h * LANES + lane) // tl == seq
        tile = jnp.where(here, jnp.broadcast_to(line, (seqs, LANES)), tile)
    tile_ref[...] = jnp.transpose(fold(tile, tl))[0:tl, :]


def post_kernel(
    dims, len_ref, prompt_ref, recv_ref, w_ref, adv_ref, ret_ref, rmask_ref,
    logprob_ref, ratio_ref, tile_ref,
    loss_hbm, grad_hbm, loss_ref, grad_ref, sems,
):
    dp, tn, rows, tl = dims
    seqs = dp * rows
    group, lane, slot = group_grid(dp, tl)
    parts = [
        [recv_ref[pl.ds(j * rows + s, dp, stride=tn * rows), :] for j in range(tn)]
        for s in range(rows)
    ]
    firsts = [part[0] for part in parts]

    columns = jnp.transpose(jnp.concatenate(firsts, axis=0))
    coeff = (
        32.0 * columns[3 * tl : 4 * tl, :] * (tile_ref[...] - columns[2 * tl : 3 * tl, :])
    )
    weights = w_ref[...][None, :].astype(F32)
    pieces = sems.shape[0] - 1
    piece = seqs // pieces
    copies = []
    for k in range(pieces):
        for b in range(k * piece, (k + 1) * piece):
            at = (b % rows) * dp + b // rows
            grad_ref[b] = (coeff[:, at : at + 1] * weights).astype(grad_ref.dtype)
        at = pl.ds(k * piece, piece)
        copies.append(pltpu.make_async_copy(grad_ref.at[at], grad_hbm.at[at], sems.at[k]))
        copies[-1].start()

    def row_of(x, k):
        apart = pltpu.roll(x, 0, 1, stride=tl, stride_axis=0)
        row = jnp.sum(jnp.where(slot == (group + k) % dp, apart, 0.0), axis=0, keepdims=True)
        return pltpu.roll(row, LANES - k * tl, 1) if k else row

    for s in range(rows):
        value_pred = row_of(sum(parts[s][1:], firsts[s]), 0)
        ref_row = row_of(firsts[s], 1)
        own = prompt_ref[s].astype(F32)
        sums = jnp.zeros((1, LANES), F32)
        for first in firsts:
            same = first[:, 4 * tl + 3 : 4 * tl + 4] == own
            sums += jnp.sum(jnp.where(same, first, 0.0), axis=0, keepdims=True)
        count = jnp.maximum(sums[:, 4 * tl : 4 * tl + 1], 1.0)
        total = sums[:, 4 * tl + 1 : 4 * tl + 2]
        mean = total / count
        var = (sums[:, 4 * tl + 2 : 4 * tl + 3] - mean * total) / count
        whitened = (adv_ref[s : s + 1, :] - mean) * lax.rsqrt(var + 1.0)

        ratio = ratio_ref[s : s + 1, :]
        surrogate = jnp.maximum(-whitened * ratio, -whitened * jnp.clip(ratio, 0.8, 1.2))
        surrogate = jnp.where(whitened < 0.0, jnp.minimum(surrogate, -3.0 * whitened), surrogate)
        drift = jnp.clip(ref_row - logprob_ref[s : s + 1, :], -20.0, 20.0)
        penalty = jnp.clip(jnp.exp(drift) - drift - 1.0, -10.0, 10.0)
        error = value_pred - ret_ref[s : s + 1, :]
        live = live_row(rmask_ref, len_ref, s)
        loss_ref[s : s + 1, :] = live * (surrogate + 0.1 * penalty + 0.25 * error * error)
    copies.append(pltpu.make_async_copy(loss_ref, loss_hbm, sems.at[pieces]))
    copies[-1].start()
    for copy in copies:
        copy.wait()


def per_device(
    logits,
    token_ids,
    response_mask,
    lengths,
    prompt_of,
    old_logprob,
    ref_logprob,
    advantages,
    returns,
    critic_hidden,
    value_weight,
):
    rows, tokens, width = logits.shape
    seqs, tl, feat = critic_hidden.shape
    dp, tn = lax.axis_size("dp"), lax.axis_size("tensor")
    dims = (dp, tn, rows, tl)
    if tokens != LANES or width % LANES or 5 * tl > LANES or LANES % tl or tn & (tn - 1):
        raise ValueError("unsupported shapes")
    smem = pl.BlockSpec(memory_space=pltpu.SMEM)
    vmem = pl.BlockSpec(memory_space=pltpu.VMEM)
    hbm = pl.BlockSpec(memory_space=pltpu.HBM)

    def grant(mib):
        return pltpu.CompilerParams(vmem_limit_bytes=mib << 20)

    stats_scratch = [
        pltpu.VMEM(logits.shape, logits.dtype),
        pltpu.VMEM((rows, tokens), jnp.int32),
        pltpu.SMEM((rows, tokens), jnp.int32),
        pltpu.VMEM((rows, tokens, LANES), F32),
        pltpu.VMEM((rows, tokens, LANES), jnp.bfloat16),
        pltpu.VMEM((rows, tokens, LANES), F32),
        pltpu.VMEM((rows, tokens, LANES), F32),
        pltpu.SemaphoreType.DMA((rows, 4)),
        pltpu.SemaphoreType.DMA((2,)),
    ]
    send, early = pl.pallas_call(
        functools.partial(pre_kernel, dims),
        name="pre",
        out_shape=(
            jax.ShapeDtypeStruct((dp * tn * rows, LANES), F32),
            jax.ShapeDtypeStruct((4 * rows, LANES), F32),
        ),
        in_specs=[hbm] * 10,
        out_specs=(hbm, vmem),
        scratch_shapes=[
            pltpu.SMEM(lengths.shape, jnp.int32),
            pltpu.SMEM(prompt_of.shape, jnp.int32),
            pltpu.VMEM((seqs * tl, feat), jnp.bfloat16),
            pltpu.VMEM((feat,), jnp.bfloat16),
            pltpu.VMEM((seqs, tl), jnp.bfloat16),
            pltpu.VMEM((rows, LANES), F32),
            pltpu.VMEM((rows, LANES), jnp.int32),
            pltpu.VMEM((rows, LANES), F32),
            pltpu.VMEM((dp * tn * rows, LANES), F32),
            pltpu.VMEM((seqs, LANES), F32),
            pltpu.SemaphoreType.DMA((9,)),
            *stats_scratch,
        ],
        compiler_params=grant(10),
    )(
        *in_hbm(
            lengths, prompt_of, critic_hidden.reshape(seqs * tl, feat), value_weight, ref_logprob,
            returns, response_mask, advantages, token_ids, logits,
        )
    )
    received = lax.all_to_all(
        send.reshape(dp * tn, rows, LANES), ("dp", "tensor"), 0, 0, tiled=True
    ).reshape(dp * tn * rows, LANES)

    stats = pl.pallas_call(
        stats_kernel,
        name="stats",
        out_shape=jax.ShapeDtypeStruct((4 * rows, LANES), F32),
        in_specs=[hbm, vmem, hbm],
        out_specs=vmem,
        scratch_shapes=stats_scratch,
        compiler_params=grant(8),
        cost_estimate=pl.CostEstimate(
            flops=8 * logits.size, bytes_accessed=2 * logits.size, transcendentals=logits.size
        ),
    )(*in_hbm(token_ids), early, *in_hbm(logits))
    shards = [stats] + [
        lax.ppermute(stats, "tensor", [(t, t ^ k) for t in range(tn)])
        for k in reversed(range(1, tn))
    ]

    merged = pl.pallas_call(
        functools.partial(merge_kernel, dims),
        name="merge",
        out_shape=(
            jax.ShapeDtypeStruct((rows, LANES), F32),
            jax.ShapeDtypeStruct((rows, LANES), F32),
            jax.ShapeDtypeStruct((tl, seqs), F32),
        ),
        in_specs=[vmem] * (1 + tn),
        out_specs=(vmem,) * 3,
        compiler_params=grant(4),
    )(old_logprob, *shards)

    return pl.pallas_call(
        functools.partial(post_kernel, dims),
        name="post",
        out_shape=(
            jax.ShapeDtypeStruct((rows, tokens), F32),
            jax.ShapeDtypeStruct((seqs, tl, feat), jnp.bfloat16),
        ),
        in_specs=[smem, smem] + [vmem] * 8,
        out_specs=(hbm, hbm),
        scratch_shapes=[
            pltpu.VMEM((rows, tokens), F32),
            pltpu.VMEM((seqs, tl, feat), jnp.bfloat16),
            pltpu.SemaphoreType.DMA((5,)),
        ],
        compiler_params=grant(6),
    )(lengths, prompt_of, received, value_weight, advantages, returns, response_mask, *merged)


def solution(mesh):
    in_specs = (
        P("dp", None, "tensor"),
        P("dp", None),
        P("dp", None),
        P("dp"),
        P("dp"),
        P("dp", None),
        P(None, "dp"),
        P("dp", None),
        P("dp", None),
        P(None, "dp", "tensor"),
        P("tensor"),
    )
    out_specs = (P("dp", None), P(None, "dp", "tensor"))
    return jax.shard_map(
        per_device, mesh=mesh, in_specs=in_specs, out_specs=out_specs, check_vma=False
    )
```

time: 22.3 us -> 21.6 us (0.969)
  the two profiles are of different devices: /device:TPU:0 before, /device:TPU:3 now
where the time goes in v3:
time: 21.6 us; the launch traced here: 21.4 us
  Pallas kernels  9.28 us (43%)
  starting transfers between devices  8.81 us (41%)
  waiting for transfers between devices  2.47 us (11%)
  between operations  0.76 us (4%)
    all_to_all x1, starting transfers between devices, per_device(): lax.all_to_all(send.reshape(dp * tn, rows, LANES), ('dp', 'tensor'), 0, 0...  6.6 us
    pallas_call x1, Pallas kernels, per_device(): pl.pallas_call(stats_kernel, name='stats', out_shape=jax.ShapeDtypeStruct...  4.86 us
    ppermute x3, waiting for transfers between devices, per_device(): lax.ppermute(stats, 'tensor', [(t, t ^ k) for t in range(tn)])  2.47 us
    pallas_call x1, Pallas kernels, per_device(): pl.pallas_call(functools.partial(pre_kernel, dims), name='pre', out_shape...  2.43 us
    ppermute x3, starting transfers between devices, per_device(): lax.ppermute(stats, 'tensor', [(t, t ^ k) for t in range(tn)])  2.21 us
    pallas_call x1, Pallas kernels, per_device(): pl.pallas_call(functools.partial(post_kernel, dims), name='post', out_sha...  1.72 us
  transfers between devices with their start and end apart: 4, of which 2 were waited for; matrix products, arithmetic and copies ran while one was open for 0% of the time, Pallas kernels for 24%

profile of v3, /device:TPU:3, one launch (start us, length us, event | category | flops | bytes accessed | tf_op | source)
XLA Modules:
  0.0 21.4 jit_solution(15287506817552173732)
XLA Ops:
  0.6 0.0 copy-start.6
  0.6 0.0 copy-start
  0.7 0.0 copy-start.1
  0.7 0.0 copy-start.2
  0.7 0.0 copy-start.3
  0.7 0.0 copy-start.4
  0.7 0.0 copy-start.5
  0.7 2.4 %pre.1 = (f32[64,128]{1,0:T(8,128)}, f32[8,128]{1,0:T(8,128)S(1)}) custom-call(s32[2]{0:T(128)} %len_ref.1, s32[2]{0:T(128)} %prompt_ref.1, bf16[256,1280]{1,0:T(8,128)(2,1)} %bitcast.4, bf16[1280]{0:T(1024)(128)(2,1)} %w_ref.1, bf16[16,16]{1,0:T(8,128)(2,1)} %refl_hbm.1, f32[2,128]{1,0:T(2,128)} %ret_ref.1, s32[2,128]{1,0:T(2,128)} %rmask_ref.1, ...), custom_call_target="tpu_custom_call" | custom-call | tf_op jit(solution)/shard_map/pre/pallas_call | solution.py:354
  3.1 6.6 %all-to-all-start = ((f32[32,2,128]{2,1,0:T(2,128)}), f32[32,2,128]{2,1,0:T(2,128)S(1)}, u32[]{:S(2)}, u32[]{:S(2)}) async-start(f32[32,2,128]{2,1,0:T(2,128)} %bitcast.1), calls=%async_computation | async-start | bytes 65536 | tf_op jit(solution)/shard_map/all_to_all | solution.py:384
  9.8 4.9 %stats.1.refs_0_ = f32[8,128]{1,0:T(8,128)S(1)} custom-call(s32[2,128]{1,0:T(2,128)} %ids_hbm.3, f32[8,128]{1,0:T(8,128)S(1)} %get-tuple-element.8.early_ref, bf16[2,128,4864]{2,1,0:T(8,128)(2,1)} %logits_hbm.3), custom_call_target="tpu_custom_call" | custom-call | flops 9961472 | bytes 2490368 | tf_op jit(solution)/shard_map/stats/pallas_call | solution.py:388
  14.6 0.5 %collective-permute-start.2 = (f32[8,128]{1,0:T(8,128)S(1)}, f32[8,128]{1,0:T(8,128)S(1)}, u32[]{:S(2)}, u32[]{:S(2)}) collective-permute-start(f32[8,128]{1,0:T(8,128)S(1)} %stats.1.refs_0_), channel_id=1, source_target_pairs={{0,1},{1,0},{2,3},{3,2},{4,5},{5,4},{6,7},{7,6},{8,9},{9,8},{10,11... | collective-permute-start | bytes 12296 | tf_op jit(solution)/shard_map/ppermute | solution.py:401
  15.1 1.2 %collective-permute-start.1 = (f32[8,128]{1,0:T(8,128)S(1)}, f32[8,128]{1,0:T(8,128)S(1)}, u32[]{:S(2)}, u32[]{:S(2)}) collective-permute-start(f32[8,128]{1,0:T(8,128)S(1)} %stats.1.refs_0_), channel_id=1, source_target_pairs={{0,2},{1,3},{2,0},{3,1},{4,6},{5,7},{6,4},{7,5},{8,10},{9,11},{10,... | collective-permute-start | bytes 12296 | tf_op jit(solution)/shard_map/ppermute | solution.py:401
  16.3 0.6 %collective-permute-start = (f32[8,128]{1,0:T(8,128)S(1)}, f32[8,128]{1,0:T(8,128)S(1)}, u32[]{:S(2)}, u32[]{:S(2)}) collective-permute-start(f32[8,128]{1,0:T(8,128)S(1)} %stats.1.refs_0_), channel_id=1, source_target_pairs={{0,3},{1,2},{2,1},{3,0},{4,7},{5,6},{6,5},{7,4},{8,11},{9,10},{10,... | collective-permute-start | bytes 12296 | tf_op jit(solution)/shard_map/ppermute | solution.py:401
  16.8 0.0 collective-permute-done.2.refs_3_
  16.8 0.7 %collective-permute-done.1.refs_2_ = f32[8,128]{1,0:T(8,128)S(1)} collective-permute-done((f32[8,128]{1,0:T(8,128)S(1)}, f32[8,128]{1,0:T(8,128)S(1)}, u32[]{:S(2)}, u32[]{:S(2)}) %collective-permute-start.1) | collective-permute-done | bytes 4128 | tf_op jit(solution)/shard_map/ppermute | solution.py:401
  17.5 1.8 %collective-permute-done.refs_1_ = f32[8,128]{1,0:T(8,128)S(1)} collective-permute-done((f32[8,128]{1,0:T(8,128)S(1)}, f32[8,128]{1,0:T(8,128)S(1)}, u32[]{:S(2)}, u32[]{:S(2)}) %collective-permute-start) | collective-permute-done | bytes 4128 | tf_op jit(solution)/shard_map/ppermute | solution.py:401
  19.3 0.0 copy-done.6
  19.3 0.3 %merge.1 = (f32[2,128]{1,0:T(2,128)S(1)}, f32[2,128]{1,0:T(2,128)S(1)}, f32[16,16]{1,0:T(8,128)S(1)}) custom-call(f32[2,128]{1,0:T(2,128)S(1)} %copy-done.6, f32[8,128]{1,0:T(8,128)S(1)} %stats.1.refs_0_, f32[8,128]{1,0:T(8,128)S(1)} %collective-permute-done.refs_1_, f32[8,128]{1,0:T(8,128)S(1)} %collective-permute-done.1.refs_2_, ...), custom_call_target="tpu_custom_call" | custom-call | tf_op jit(solution)/shard_map/merge/pallas_call | solution.py:405
  19.6 0.0 all-to-all-done
  19.6 0.0 copy-done
  19.6 0.0 copy-done.1
  19.6 0.0 copy-done.2
  19.6 0.0 copy-done.3
  19.6 1.7 %post.1 = (f32[2,128]{1,0:T(2,128)}, bf16[16,16,1280]{2,1,0:T(8,128)(2,1)}) custom-call(s32[2]{0:T(128)S(1)} %copy-done.4, s32[2]{0:T(128)S(1)} %copy-done.5, f32[64,128]{1,0:T(8,128)S(1)} %bitcast.3, bf16[1280]{0:T(1024)(128)(2,1)S(1)} %copy-done, f32[2,128]{1,0:T(2,128)S(1)} %copy-done.3, f32[2,128]{1,0:T(2,128)S(1)} %copy-done.1, s32[2,128]{1,0:T(2,128)S(1)} %copy-done.2, ...), custom_call_target="tpu_custom_call" | custom-call | tf_op jit(solution)/shard_map/post/pallas_call | solution.py:418
  (2 shorter events, 0.0 us)
Async XLA Ops:
  0.6 18.7 %copy-start.6 = (f32[2,128]{1,0:T(2,128)S(1)}, f32[2,128]{1,0:T(2,128)}, u32[]{:S(2)}) copy-start(f32[2,128]{1,0:T(2,128)} %old_ref.1) | copy-start | bytes 3076
  0.6 18.9 %copy-start = (bf16[1280]{0:T(1024)(128)(2,1)S(1)}, bf16[1280]{0:T(1024)(128)(2,1)}, u32[]{:S(2)}) copy-start(bf16[1280]{0:T(1024)(128)(2,1)} %w_ref.1) | copy-start | bytes 7684
  0.7 18.9 %copy-start.1 = (f32[2,128]{1,0:T(2,128)S(1)}, f32[2,128]{1,0:T(2,128)}, u32[]{:S(2)}) copy-start(f32[2,128]{1,0:T(2,128)} %ret_ref.1) | copy-start | bytes 3076
  0.7 18.9 %copy-start.2 = (s32[2,128]{1,0:T(2,128)S(1)}, s32[2,128]{1,0:T(2,128)}, u32[]{:S(2)}) copy-start(s32[2,128]{1,0:T(2,128)} %rmask_ref.1) | copy-start | bytes 3076
  0.7 18.9 %copy-start.3 = (f32[2,128]{1,0:T(2,128)S(1)}, f32[2,128]{1,0:T(2,128)}, u32[]{:S(2)}) copy-start(f32[2,128]{1,0:T(2,128)} %adv_ref.1) | copy-start | bytes 3076
  0.7 18.9 %copy-start.4 = (s32[2]{0:T(128)S(1)}, s32[2]{0:T(128)}, u32[]{:S(2)}) copy-start(s32[2]{0:T(128)} %len_ref.1) | copy-start | bytes 28
  0.7 18.9 %copy-start.5 = (s32[2]{0:T(128)S(1)}, s32[2]{0:T(128)}, u32[]{:S(2)}) copy-start(s32[2]{0:T(128)} %prompt_ref.1) | copy-start | bytes 28
  3.1 16.4 %all-to-all-start = ((f32[32,2,128]{2,1,0:T(2,128)}), f32[32,2,128]{2,1,0:T(2,128)S(1)}, u32[]{:S(2)}, u32[]{:S(2)}) async-start(f32[32,2,128]{2,1,0:T(2,128)} %bitcast.1), calls=%async_computation | async-start | bytes 65536 | tf_op jit(solution)/shard_map/all_to_all | solution.py:384
  14.6 2.2 %collective-permute-start.2 = (f32[8,128]{1,0:T(8,128)S(1)}, f32[8,128]{1,0:T(8,128)S(1)}, u32[]{:S(2)}, u32[]{:S(2)}) collective-permute-start(f32[8,128]{1,0:T(8,128)S(1)} %stats.1.refs_0_), channel_id=1, source_target_pairs={{0,1},{1,0},{2,3},{3,2},{4,5},{5,4},{6,7},{7,6},{8,9},{9,8},{10,11... | collective-permute-start | bytes 12296 | tf_op jit(solution)/shard_map/ppermute | solution.py:401
  15.1 2.5 %collective-permute-start.1 = (f32[8,128]{1,0:T(8,128)S(1)}, f32[8,128]{1,0:T(8,128)S(1)}, u32[]{:S(2)}, u32[]{:S(2)}) collective-permute-start(f32[8,128]{1,0:T(8,128)S(1)} %stats.1.refs_0_), channel_id=1, source_target_pairs={{0,2},{1,3},{2,0},{3,1},{4,6},{5,7},{6,4},{7,5},{8,10},{9,11},{10,... | collective-permute-start | bytes 12296 | tf_op jit(solution)/shard_map/ppermute | solution.py:401
  16.3 3.0 %collective-permute-start = (f32[8,128]{1,0:T(8,128)S(1)}, f32[8,128]{1,0:T(8,128)S(1)}, u32[]{:S(2)}, u32[]{:S(2)}) collective-permute-start(f32[8,128]{1,0:T(8,128)S(1)} %stats.1.refs_0_), channel_id=1, source_target_pairs={{0,3},{1,2},{2,1},{3,0},{4,7},{5,6},{6,5},{7,4},{8,11},{9,10},{10,... | collective-permute-start | bytes 12296 | tf_op jit(solution)/shard_map/ppermute | solution.py:401

commit v4 on v3

--- a/solution.py
+++ b/solution.py
@@ -8,6 +8,7 @@
 from jax.sharding import PartitionSpec as P
 
 LANES = 128
+STEPS = 4
 F32 = jnp.float32
 
 
@@ -53,7 +54,7 @@
 def pre_kernel(
     dims, len_hbm, prompt_hbm, critic_hbm, w_hbm, refl_hbm, ret_hbm, rmask_hbm, adv_hbm,
     ids_hbm, logits_hbm,
-    send_hbm, stats_ref,
+    send_hbm, stats_ref, local_ref,
     len_ref, prompt_ref, critic_ref, w_ref, reflp_ref, ret_ref, rmask_ref, adv_ref, send_ref,
     wide_ref, sems, *scratch,
 ):
@@ -69,21 +70,29 @@
         copy.wait()
     wide_ref[:, 0:tl] = reflp_ref[...].astype(F32)
     group, lane, slot = group_grid(dp, tl)
+    place = (lane - group * (rows * tl)) & (LANES - 1)
+    spot = place // tl
     blocks = []
     for s in range(rows):
         live = live_row(rmask_ref, len_ref, s)
         adv = adv_ref[s : s + 1, :]
         gain = live * adv
-        refs = pltpu.roll(wide_ref[pl.ds(s, dp, stride=rows), :], tl, 1)
+        prompt = prompt_ref[s].astype(F32)
+        local_ref[s : s + 1, :] = live
+        local_ref[rows + s : rows + s + 1, :] = jnp.zeros((1, LANES), F32) + prompt
+        local_ref[2 * rows + s : 2 * rows + s + 1, :] = adv
+        local_ref[3 * rows + s : 3 * rows + s + 1, :] = ret_ref[s : s + 1, :]
+        refs = jnp.where(slot == 0, wide_ref[pl.ds(s, dp, stride=rows), :], 0.0)
         rets = jnp.where(slot == group, jnp.broadcast_to(ret_ref[s : s + 1, :], (dp, LANES)), 0.0)
         lives = jnp.where(slot == group, jnp.broadcast_to(live, (dp, LANES)), 0.0)
-        block = jnp.where(slot == 1, refs, 0.0)
-        block = jnp.where(slot == 2, fold(rets, tl), block)
-        block = jnp.where(slot == 3, fold(lives, tl), block)
-        block = jnp.where(lane == 4 * tl, jnp.sum(live, axis=1, keepdims=True), block)
-        block = jnp.where(lane == 4 * tl + 1, jnp.sum(gain, axis=1, keepdims=True), block)
-        block = jnp.where(lane == 4 * tl + 2, jnp.sum(gain * adv, axis=1, keepdims=True), block)
-        block = jnp.where(lane == 4 * tl + 3, prompt_ref[s].astype(F32), block)
+        block = jnp.where(spot == rows, fold(refs, tl), 0.0)
+        block = jnp.where(spot == rows + 1, fold(rets, tl), block)
+        block = jnp.where(spot == rows + 2, fold(lives, tl), block)
+        last = (rows + 3) * tl
+        block = jnp.where(place == last, jnp.sum(live, axis=1, keepdims=True), block)
+        block = jnp.where(place == last + 1, jnp.sum(gain, axis=1, keepdims=True), block)
+        block = jnp.where(place == last + 2, jnp.sum(gain * adv, axis=1, keepdims=True), block)
+        block = jnp.where(place == last + 3, prompt, block)
         blocks.append(block)
     for copy in copies[:2]:
         copy.wait()
@@ -95,43 +104,42 @@
     for h in range(rows):
         stats_ref[3 * rows + h : 3 * rows + h + 1, :] = flat[h]
     for s in range(rows):
-        value = jnp.zeros((dp, LANES), F32)
+        block = blocks[s]
         for h in range(rows):
             line = jnp.broadcast_to(flat[h], (dp, LANES))
-            value = jnp.where((h * LANES + lane) // tl == group * rows + s, line, value)
-        block = jnp.where(slot == 0, fold(value, tl), blocks[s])
+            block = jnp.where((h * LANES + lane) // tl == group * rows + s, line, block)
         for j in range(tn):
             send_ref[pl.ds(j * rows + s, dp, stride=tn * rows), :] = block
-    out = pltpu.make_async_copy(send_ref, send_hbm, sems.at[len(pairs)])
+    out = pltpu.make_async_copy(send_ref, send_hbm, sems.at[sems.shape[0] - 1])
     out.start()
 
     @pl.when(is_early())
     def _():
-        run_stats(ids_hbm, logits_hbm, stats_ref, *scratch)
+        run_stats(ids_hbm, logits_hbm, stats_ref, *scratch, sems)
 
     out.wait()
 
 
 def run_stats(
     ids_hbm, logits_hbm, out_ref,
-    logits_ref, ids_ref, ids_smem, here_ref, top_ref, sum_ref, hit_ref, sems, ids_sems,
+    logits_ref, ids_ref, ids_smem, here_ref, top_ref, sum_ref, hit_ref, sems,
 ):
     rows, tokens, width = logits_ref.shape
     chunks = width // LANES
-    steps = sems.shape[1]
+    steps = STEPS
     step = tokens // steps
     blocks = [(s, k) for s in range(rows) for k in range(steps)]
     copies = [
         pltpu.make_async_copy(
             logits_hbm.at[s, pl.ds(k * step, step)],
             logits_ref.at[s, pl.ds(k * step, step)],
-            sems.at[s, k],
+            sems.at[s * steps + k],
         )
         for s, k in blocks
     ]
     ids_copies = [
-        pltpu.make_async_copy(ids_hbm, ids_ref, ids_sems.at[0]),
-        pltpu.make_async_copy(ids_hbm, ids_smem, ids_sems.at[1]),
+        pltpu.make_async_copy(ids_hbm, ids_ref, sems.at[rows * steps]),
+        pltpu.make_async_copy(ids_hbm, ids_smem, sems.at[rows * steps + 1]),
     ]
     for copy in ids_copies + copies:
         copy.start()
@@ -252,8 +260,7 @@
 
 
 def post_kernel(
-    dims, len_ref, prompt_ref, recv_ref, w_ref, adv_ref, ret_ref, rmask_ref,
-    logprob_ref, ratio_ref, tile_ref,
+    dims, recv_ref, w_ref, local_ref, logprob_ref, ratio_ref, tile_ref,
     loss_hbm, grad_hbm, loss_ref, grad_ref, sems,
 ):
     dp, tn, rows, tl = dims
@@ -263,11 +270,22 @@
         [recv_ref[pl.ds(j * rows + s, dp, stride=tn * rows), :] for j in range(tn)]
         for s in range(rows)
     ]
-    firsts = [part[0] for part in parts]
+    back = LANES - (lax.axis_index("dp") * (rows * tl)) % LANES
+    firsts = [pltpu.roll(part[0], back, 1) for part in parts]
+    every = [pltpu.roll(sum(part[1:], part[0]), back, 1) for part in parts]
+
+    def row_of(x, k):
+        apart = pltpu.roll(x, 0, 1, stride=tl, stride_axis=0)
+        row = jnp.sum(jnp.where(slot == (group + k) % dp, apart, 0.0), axis=0, keepdims=True)
+        return pltpu.roll(row, LANES - k * tl, 1) if k else row
+
+    spot = (rows + 3) * tl
+    prompts = [first[:, spot + 3 : spot + 4] for first in firsts]
 
     columns = jnp.transpose(jnp.concatenate(firsts, axis=0))
+    at = (rows + 1) * tl
     coeff = (
-        32.0 * columns[3 * tl : 4 * tl, :] * (tile_ref[...] - columns[2 * tl : 3 * tl, :])
+        32.0 * columns[at + tl : at + 2 * tl, :] * (tile_ref[...] - columns[at : at + tl, :])
     )
     weights = w_ref[...][None, :].astype(F32)
     pieces = sems.shape[0] - 1
@@ -281,32 +299,28 @@
         copies.append(pltpu.make_async_copy(grad_ref.at[at], grad_hbm.at[at], sems.at[k]))
         copies[-1].start()
 
-    def row_of(x, k):
-        apart = pltpu.roll(x, 0, 1, stride=tl, stride_axis=0)
-        row = jnp.sum(jnp.where(slot == (group + k) % dp, apart, 0.0), axis=0, keepdims=True)
-        return pltpu.roll(row, LANES - k * tl, 1) if k else row
-
     for s in range(rows):
-        value_pred = row_of(sum(parts[s][1:], firsts[s]), 0)
-        ref_row = row_of(firsts[s], 1)
-        own = prompt_ref[s].astype(F32)
+        value_pred = row_of(every[s], s)
+        ref_row = row_of(firsts[s], rows)
+        own = local_ref[rows + s : rows + s + 1, 0:1]
         sums = jnp.zeros((1, LANES), F32)
-        for first in firsts:
-            same = first[:, 4 * tl + 3 : 4 * tl + 4] == own
-            sums += jnp.sum(jnp.where(same, first, 0.0), axis=0, keepdims=True)
-        count = jnp.maximum(sums[:, 4 * tl : 4 * tl + 1], 1.0)
-        total = sums[:, 4 * tl + 1 : 4 * tl + 2]
+        for first, prompt in zip(firsts, prompts):
+            sums += jnp.sum(jnp.where(prompt == own, first, 0.0), axis=0, keepdims=True)
+        count = jnp.maximum(sums, 1.0)
+        total = pltpu.roll(sums, LANES - 1, 1)
+        square = pltpu.roll(sums, LANES - 2, 1)
         mean = total / count
-        var = (sums[:, 4 * tl + 2 : 4 * tl + 3] - mean * total) / count
-        whitened = (adv_ref[s : s + 1, :] - mean) * lax.rsqrt(var + 1.0)
+        scale = lax.rsqrt((square - mean * total) / count + 1.0)
+        adv = local_ref[2 * rows + s : 2 * rows + s + 1, :]
+        whitened = (adv - mean[:, spot : spot + 1]) * scale[:, spot : spot + 1]
 
         ratio = ratio_ref[s : s + 1, :]
         surrogate = jnp.maximum(-whitened * ratio, -whitened * jnp.clip(ratio, 0.8, 1.2))
         surrogate = jnp.where(whitened < 0.0, jnp.minimum(surrogate, -3.0 * whitened), surrogate)
         drift = jnp.clip(ref_row - logprob_ref[s : s + 1, :], -20.0, 20.0)
         penalty = jnp.clip(jnp.exp(drift) - drift - 1.0, -10.0, 10.0)
-        error = value_pred - ret_ref[s : s + 1, :]
-        live = live_row(rmask_ref, len_ref, s)
+        error = value_pred - local_ref[3 * rows + s : 3 * rows + s + 1, :]
+        live = local_ref[s : s + 1, :]
         loss_ref[s : s + 1, :] = live * (surrogate + 0.1 * penalty + 0.25 * error * error)
     copies.append(pltpu.make_async_copy(loss_ref, loss_hbm, sems.at[pieces]))
     copies[-1].start()
@@ -331,9 +345,8 @@
     seqs, tl, feat = critic_hidden.shape
     dp, tn = lax.axis_size("dp"), lax.axis_size("tensor")
     dims = (dp, tn, rows, tl)
-    if tokens != LANES or width % LANES or 5 * tl > LANES or LANES % tl or tn & (tn - 1):
+    if tokens != LANES or width % LANES or (rows + 3) * tl + 4 > LANES or LANES % tl or tn & (tn - 1):
         raise ValueError("unsupported shapes")
-    smem = pl.BlockSpec(memory_space=pltpu.SMEM)
     vmem = pl.BlockSpec(memory_space=pltpu.VMEM)
     hbm = pl.BlockSpec(memory_space=pltpu.HBM)
 
@@ -348,18 +361,18 @@
         pltpu.VMEM((rows, tokens, LANES), jnp.bfloat16),
         pltpu.VMEM((rows, tokens, LANES), F32),
         pltpu.VMEM((rows, tokens, LANES), F32),
-        pltpu.SemaphoreType.DMA((rows, 4)),
-        pltpu.SemaphoreType.DMA((2,)),
     ]
-    send, early = pl.pallas_call(
+    copies = rows * STEPS + 2
+    send, early, local = pl.pallas_call(
         functools.partial(pre_kernel, dims),
         name="pre",
         out_shape=(
             jax.ShapeDtypeStruct((dp * tn * rows, LANES), F32),
             jax.ShapeDtypeStruct((4 * rows, LANES), F32),
+            jax.ShapeDtypeStruct((4 * rows, LANES), F32),
         ),
         in_specs=[hbm] * 10,
-        out_specs=(hbm, vmem),
+        out_specs=(hbm, vmem, vmem),
         scratch_shapes=[
             pltpu.SMEM(lengths.shape, jnp.int32),
             pltpu.SMEM(prompt_of.shape, jnp.int32),
@@ -371,7 +384,7 @@
             pltpu.VMEM((rows, LANES), F32),
             pltpu.VMEM((dp * tn * rows, LANES), F32),
             pltpu.VMEM((seqs, LANES), F32),
-            pltpu.SemaphoreType.DMA((9,)),
+            pltpu.SemaphoreType.DMA((max(copies, 8) + 1,)),
             *stats_scratch,
         ],
         compiler_params=grant(10),
@@ -391,7 +404,7 @@
         out_shape=jax.ShapeDtypeStruct((4 * rows, LANES), F32),
         in_specs=[hbm, vmem, hbm],
         out_specs=vmem,
-        scratch_shapes=stats_scratch,
+        scratch_shapes=[*stats_scratch, pltpu.SemaphoreType.DMA((copies,))],
         compiler_params=grant(8),
         cost_estimate=pl.CostEstimate(
             flops=8 * logits.size, bytes_accessed=2 * logits.size, transcendentals=logits.size
@@ -422,15 +435,15 @@
             jax.ShapeDtypeStruct((rows, tokens), F32),
             jax.ShapeDtypeStruct((seqs, tl, feat), jnp.bfloat16),
         ),
-        in_specs=[smem, smem] + [vmem] * 8,
+        in_specs=[vmem] * 6,
         out_specs=(hbm, hbm),
         scratch_shapes=[
             pltpu.VMEM((rows, tokens), F32),
             pltpu.VMEM((seqs, tl, feat), jnp.bfloat16),
-            pltpu.SemaphoreType.DMA((5,)),
+            pltpu.SemaphoreType.DMA((3,)),
         ],
         compiler_params=grant(6),
-    )(lengths, prompt_of, received, value_weight, advantages, returns, response_mask, *merged)
+    )(received, value_weight, local, *merged)
 
 
 def solution(mesh):

time: 21.6 us -> 20.1 us (0.931)
  Pallas kernels: 9.28 us -> 8.08 us
    pallas_call x1, Pallas kernels: 1.72 us -> 1.2 us  [per_device(): pl.pallas_call(functools.partial(post_kernel, dims), name='post', out_sha...]
    pallas_call x1, Pallas kernels: 4.86 us -> 4.49 us  [per_device(): pl.pallas_call(stats_kernel, name='stats', out_shape=jax.ShapeDtypeStruct...]
    pallas_call x1, Pallas kernels: 2.43 us -> 2.12 us  [per_device(): pl.pallas_call(functools.partial(pre_kernel, dims), name='pre', out_shape...]
where the time goes in v4:
time: 20.1 us; the launch traced here: 19.9 us
  starting transfers between devices  8.62 us (43%)
  Pallas kernels  8.08 us (40%)
  waiting for transfers between devices  2.47 us (12%)
  between operations  0.68 us (3%)
    all_to_all x1, starting transfers between devices, per_device(): lax.all_to_all(send.reshape(dp * tn, rows, LANES), ('dp', 'tensor'), 0, 0...  6.41 us
    pallas_call x1, Pallas kernels, per_device(): pl.pallas_call(stats_kernel, name='stats', out_shape=jax.ShapeDtypeStruct...  4.49 us
    ppermute x3, waiting for transfers between devices, per_device(): lax.ppermute(stats, 'tensor', [(t, t ^ k) for t in range(tn)])  2.47 us
    ppermute x3, starting transfers between devices, per_device(): lax.ppermute(stats, 'tensor', [(t, t ^ k) for t in range(tn)])  2.21 us
    pallas_call x1, Pallas kernels, per_device(): pl.pallas_call(functools.partial(pre_kernel, dims), name='pre', out_shape...  2.12 us
    pallas_call x1, Pallas kernels, per_device(): pl.pallas_call(functools.partial(post_kernel, dims), name='post', out_sha...  1.2 us
  transfers between devices with their start and end apart: 4, of which 2 were waited for; matrix products, arithmetic and copies ran while one was open for 0% of the time, Pallas kernels for 24%

profile of v4, /device:TPU:3, one launch (start us, length us, event | category | flops | bytes accessed | tf_op | source)
XLA Modules:
  0.0 19.9 jit_solution(1921562234696465632)
XLA Ops:
  0.6 0.0 copy-start.1
  0.6 0.0 copy-start
  0.7 2.1 %pre.1 = (f32[64,128]{1,0:T(8,128)}, f32[8,128]{1,0:T(8,128)S(1)}, f32[8,128]{1,0:T(8,128)S(1)}) custom-call(s32[2]{0:T(128)} %len_hbm.1, s32[2]{0:T(128)} %prompt_hbm.1, bf16[256,1280]{1,0:T(8,128)(2,1)} %bitcast.4, bf16[1280]{0:T(1024)(128)(2,1)} %w_ref.1, bf16[16,16]{1,0:T(8,128)(2,1)} %refl_hbm.1, f32[2,128]{1,0:T(2,128)} %ret_hbm.1, ...), custom_call_target="tpu_custom_call" | custom-call | tf_op jit(solution)/shard_map/pre/pallas_call | solution.py:366
  2.8 6.4 %all-to-all-start = ((f32[32,2,128]{2,1,0:T(2,128)}), f32[32,2,128]{2,1,0:T(2,128)S(1)}, u32[]{:S(2)}, u32[]{:S(2)}) async-start(f32[32,2,128]{2,1,0:T(2,128)} %bitcast.1), calls=%async_computation | async-start | bytes 65536 | tf_op jit(solution)/shard_map/all_to_all | solution.py:397
  9.2 4.5 %stats.1.refs_0_ = f32[8,128]{1,0:T(8,128)S(1)} custom-call(s32[2,128]{1,0:T(2,128)} %ids_hbm.3, f32[8,128]{1,0:T(8,128)S(1)} %get-tuple-element.10.early_ref, bf16[2,128,4864]{2,1,0:T(8,128)(2,1)} %logits_hbm.3), custom_call_target="tpu_custom_call" | custom-call | flops 9961472 | bytes 2490368 | tf_op jit(solution)/shard_map/stats/pallas_call | solution.py:401
  13.7 0.5 %collective-permute-start.2 = (f32[8,128]{1,0:T(8,128)S(1)}, f32[8,128]{1,0:T(8,128)S(1)}, u32[]{:S(2)}, u32[]{:S(2)}) collective-permute-start(f32[8,128]{1,0:T(8,128)S(1)} %stats.1.refs_0_), channel_id=1, source_target_pairs={{0,1},{1,0},{2,3},{3,2},{4,5},{5,4},{6,7},{7,6},{8,9},{9,8},{10,11... | collective-permute-start | bytes 12296 | tf_op jit(solution)/shard_map/ppermute | solution.py:414
  14.2 1.2 %collective-permute-start.1 = (f32[8,128]{1,0:T(8,128)S(1)}, f32[8,128]{1,0:T(8,128)S(1)}, u32[]{:S(2)}, u32[]{:S(2)}) collective-permute-start(f32[8,128]{1,0:T(8,128)S(1)} %stats.1.refs_0_), channel_id=1, source_target_pairs={{0,2},{1,3},{2,0},{3,1},{4,6},{5,7},{6,4},{7,5},{8,10},{9,11},{10,... | collective-permute-start | bytes 12296 | tf_op jit(solution)/shard_map/ppermute | solution.py:414
  15.3 0.6 %collective-permute-start = (f32[8,128]{1,0:T(8,128)S(1)}, f32[8,128]{1,0:T(8,128)S(1)}, u32[]{:S(2)}, u32[]{:S(2)}) collective-permute-start(f32[8,128]{1,0:T(8,128)S(1)} %stats.1.refs_0_), channel_id=1, source_target_pairs={{0,3},{1,2},{2,1},{3,0},{4,7},{5,6},{6,5},{7,4},{8,11},{9,10},{10,... | collective-permute-start | bytes 12296 | tf_op jit(solution)/shard_map/ppermute | solution.py:414
  15.9 0.0 collective-permute-done.2.refs_3_
  15.9 0.7 %collective-permute-done.1.refs_2_ = f32[8,128]{1,0:T(8,128)S(1)} collective-permute-done((f32[8,128]{1,0:T(8,128)S(1)}, f32[8,128]{1,0:T(8,128)S(1)}, u32[]{:S(2)}, u32[]{:S(2)}) %collective-permute-start.1) | collective-permute-done | bytes 4128 | tf_op jit(solution)/shard_map/ppermute | solution.py:414
  16.6 1.8 %collective-permute-done.refs_1_ = f32[8,128]{1,0:T(8,128)S(1)} collective-permute-done((f32[8,128]{1,0:T(8,128)S(1)}, f32[8,128]{1,0:T(8,128)S(1)}, u32[]{:S(2)}, u32[]{:S(2)}) %collective-permute-start) | collective-permute-done | bytes 4128 | tf_op jit(solution)/shard_map/ppermute | solution.py:414
  18.4 0.0 copy-done.1
  18.4 0.3 %merge.1 = (f32[2,128]{1,0:T(2,128)S(1)}, f32[2,128]{1,0:T(2,128)S(1)}, f32[16,16]{1,0:T(8,128)S(1)}) custom-call(f32[2,128]{1,0:T(2,128)S(1)} %copy-done.1, f32[8,128]{1,0:T(8,128)S(1)} %stats.1.refs_0_, f32[8,128]{1,0:T(8,128)S(1)} %collective-permute-done.refs_1_, f32[8,128]{1,0:T(8,128)S(1)} %collective-permute-done.1.refs_2_, ...), custom_call_target="tpu_custom_call" | custom-call | tf_op jit(solution)/shard_map/merge/pallas_call | solution.py:418
  18.7 0.0 all-to-all-done
  18.7 0.0 copy-done
  18.7 1.2 %post.1 = (f32[2,128]{1,0:T(2,128)}, bf16[16,16,1280]{2,1,0:T(8,128)(2,1)}) custom-call(f32[64,128]{1,0:T(8,128)S(1)} %bitcast.3, bf16[1280]{0:T(1024)(128)(2,1)S(1)} %copy-done, f32[8,128]{1,0:T(8,128)S(1)} %get-tuple-element.9.local_ref, f32[2,128]{1,0:T(2,128)S(1)} %get-tuple-element.11.logprob_ref, f32[2,128]{1,0:T(2,128)S(1)} %get-tuple-element.12.ratio_ref, ...), custom_call_target="tpu_custom_call" | custom-call | tf_op jit(solution)/shard_map/post/pallas_call | solution.py:431
Async XLA Ops:
  0.6 17.8 %copy-start.1 = (f32[2,128]{1,0:T(2,128)S(1)}, f32[2,128]{1,0:T(2,128)}, u32[]{:S(2)}) copy-start(f32[2,128]{1,0:T(2,128)} %old_ref.1) | copy-start | bytes 3076
  0.6 18.0 %copy-start = (bf16[1280]{0:T(1024)(128)(2,1)S(1)}, bf16[1280]{0:T(1024)(128)(2,1)}, u32[]{:S(2)}) copy-start(bf16[1280]{0:T(1024)(128)(2,1)} %w_ref.1) | copy-start | bytes 7684
  2.8 15.9 %all-to-all-start = ((f32[32,2,128]{2,1,0:T(2,128)}), f32[32,2,128]{2,1,0:T(2,128)S(1)}, u32[]{:S(2)}, u32[]{:S(2)}) async-start(f32[32,2,128]{2,1,0:T(2,128)} %bitcast.1), calls=%async_computation | async-start | bytes 65536 | tf_op jit(solution)/shard_map/all_to_all | solution.py:397
  13.7 2.2 %collective-permute-start.2 = (f32[8,128]{1,0:T(8,128)S(1)}, f32[8,128]{1,0:T(8,128)S(1)}, u32[]{:S(2)}, u32[]{:S(2)}) collective-permute-start(f32[8,128]{1,0:T(8,128)S(1)} %stats.1.refs_0_), channel_id=1, source_target_pairs={{0,1},{1,0},{2,3},{3,2},{4,5},{5,4},{6,7},{7,6},{8,9},{9,8},{10,11... | collective-permute-start | bytes 12296 | tf_op jit(solution)/shard_map/ppermute | solution.py:414
  14.2 2.5 %collective-permute-start.1 = (f32[8,128]{1,0:T(8,128)S(1)}, f32[8,128]{1,0:T(8,128)S(1)}, u32[]{:S(2)}, u32[]{:S(2)}) collective-permute-start(f32[8,128]{1,0:T(8,128)S(1)} %stats.1.refs_0_), channel_id=1, source_target_pairs={{0,2},{1,3},{2,0},{3,1},{4,6},{5,7},{6,4},{7,5},{8,10},{9,11},{10,... | collective-permute-start | bytes 12296 | tf_op jit(solution)/shard_map/ppermute | solution.py:414
  15.3 3.0 %collective-permute-start = (f32[8,128]{1,0:T(8,128)S(1)}, f32[8,128]{1,0:T(8,128)S(1)}, u32[]{:S(2)}, u32[]{:S(2)}) collective-permute-start(f32[8,128]{1,0:T(8,128)S(1)} %stats.1.refs_0_), channel_id=1, source_target_pairs={{0,3},{1,2},{2,1},{3,0},{4,7},{5,6},{6,5},{7,4},{8,11},{9,10},{10,... | collective-permute-start | bytes 12296 | tf_op jit(solution)/shard_map/ppermute | solution.py:414

commit v5 on v4

--- a/solution.py
+++ b/solution.py
@@ -64,7 +64,7 @@
         (ret_hbm, ret_ref), (refl_hbm, reflp_ref), (len_hbm, len_ref), (prompt_hbm, prompt_ref),
     )
     copies = [pltpu.make_async_copy(a, b, sems.at[k]) for k, (a, b) in enumerate(pairs)]
-    for copy in copies:
+    for copy in copies[::-1]:
         copy.start()
     for copy in copies[2:]:
         copy.wait()

time: 20.1 us -> 20 us (level)
  no operation moved by 1% of the time
where the time goes in v5:
time: 20 us; the launch traced here: 19.8 us
  starting transfers between devices  8.62 us (43%)
  Pallas kernels  8.05 us (40%)
  waiting for transfers between devices  2.47 us (12%)
  between operations  0.68 us (3%)
    all_to_all x1, starting transfers between devices, per_device(): lax.all_to_all(send.reshape(dp * tn, rows, LANES), ('dp', 'tensor'), 0, 0...  6.41 us
    pallas_call x1, Pallas kernels, per_device(): pl.pallas_call(stats_kernel, name='stats', out_shape=jax.ShapeDtypeStruct...  4.49 us
    ppermute x3, waiting for transfers between devices, per_device(): lax.ppermute(stats, 'tensor', [(t, t ^ k) for t in range(tn)])  2.47 us
    ppermute x3, starting transfers between devices, per_device(): lax.ppermute(stats, 'tensor', [(t, t ^ k) for t in range(tn)])  2.21 us
    pallas_call x1, Pallas kernels, per_device(): pl.pallas_call(functools.partial(pre_kernel, dims), name='pre', out_shape...  2.09 us
    pallas_call x1, Pallas kernels, per_device(): pl.pallas_call(functools.partial(post_kernel, dims), name='post', out_sha...  1.2 us
  transfers between devices with their start and end apart: 4, of which 2 were waited for; matrix products, arithmetic and copies ran while one was open for 0% of the time, Pallas kernels for 24%

profile of v5, /device:TPU:3, one launch (start us, length us, event | category | flops | bytes accessed | tf_op | source)
XLA Modules:
  0.0 19.8 jit_solution(6721586956681531869)
XLA Ops:
  0.6 0.0 copy-start.1
  0.6 0.0 copy-start
  0.7 2.1 %pre.1 = (f32[64,128]{1,0:T(8,128)}, f32[8,128]{1,0:T(8,128)S(1)}, f32[8,128]{1,0:T(8,128)S(1)}) custom-call(s32[2]{0:T(128)} %len_hbm.1, s32[2]{0:T(128)} %prompt_hbm.1, bf16[256,1280]{1,0:T(8,128)(2,1)} %bitcast.4, bf16[1280]{0:T(1024)(128)(2,1)} %w_ref.1, bf16[16,16]{1,0:T(8,128)(2,1)} %refl_hbm.1, f32[2,128]{1,0:T(2,128)} %ret_hbm.1, ...), custom_call_target="tpu_custom_call" | custom-call | tf_op jit(solution)/shard_map/pre/pallas_call | solution.py:366
  2.7 6.4 %all-to-all-start = ((f32[32,2,128]{2,1,0:T(2,128)}), f32[32,2,128]{2,1,0:T(2,128)S(1)}, u32[]{:S(2)}, u32[]{:S(2)}) async-start(f32[32,2,128]{2,1,0:T(2,128)} %bitcast.1), calls=%async_computation | async-start | bytes 65536 | tf_op jit(solution)/shard_map/all_to_all | solution.py:397
  9.2 4.5 %stats.1.refs_0_ = f32[8,128]{1,0:T(8,128)S(1)} custom-call(s32[2,128]{1,0:T(2,128)} %ids_hbm.3, f32[8,128]{1,0:T(8,128)S(1)} %get-tuple-element.10.early_ref, bf16[2,128,4864]{2,1,0:T(8,128)(2,1)} %logits_hbm.3), custom_call_target="tpu_custom_call" | custom-call | flops 9961472 | bytes 2490368 | tf_op jit(solution)/shard_map/stats/pallas_call | solution.py:401
  13.7 0.5 %collective-permute-start.2 = (f32[8,128]{1,0:T(8,128)S(1)}, f32[8,128]{1,0:T(8,128)S(1)}, u32[]{:S(2)}, u32[]{:S(2)}) collective-permute-start(f32[8,128]{1,0:T(8,128)S(1)} %stats.1.refs_0_), channel_id=1, source_target_pairs={{0,1},{1,0},{2,3},{3,2},{4,5},{5,4},{6,7},{7,6},{8,9},{9,8},{10,11... | collective-permute-start | bytes 12296 | tf_op jit(solution)/shard_map/ppermute | solution.py:414
  14.1 1.2 %collective-permute-start.1 = (f32[8,128]{1,0:T(8,128)S(1)}, f32[8,128]{1,0:T(8,128)S(1)}, u32[]{:S(2)}, u32[]{:S(2)}) collective-permute-start(f32[8,128]{1,0:T(8,128)S(1)} %stats.1.refs_0_), channel_id=1, source_target_pairs={{0,2},{1,3},{2,0},{3,1},{4,6},{5,7},{6,4},{7,5},{8,10},{9,11},{10,... | collective-permute-start | bytes 12296 | tf_op jit(solution)/shard_map/ppermute | solution.py:414
  15.3 0.6 %collective-permute-start = (f32[8,128]{1,0:T(8,128)S(1)}, f32[8,128]{1,0:T(8,128)S(1)}, u32[]{:S(2)}, u32[]{:S(2)}) collective-permute-start(f32[8,128]{1,0:T(8,128)S(1)} %stats.1.refs_0_), channel_id=1, source_target_pairs={{0,3},{1,2},{2,1},{3,0},{4,7},{5,6},{6,5},{7,4},{8,11},{9,10},{10,... | collective-permute-start | bytes 12296 | tf_op jit(solution)/shard_map/ppermute | solution.py:414
  15.9 0.0 collective-permute-done.2.refs_3_
  15.9 0.7 %collective-permute-done.1.refs_2_ = f32[8,128]{1,0:T(8,128)S(1)} collective-permute-done((f32[8,128]{1,0:T(8,128)S(1)}, f32[8,128]{1,0:T(8,128)S(1)}, u32[]{:S(2)}, u32[]{:S(2)}) %collective-permute-start.1) | collective-permute-done | bytes 4128 | tf_op jit(solution)/shard_map/ppermute | solution.py:414
  16.6 1.8 %collective-permute-done.refs_1_ = f32[8,128]{1,0:T(8,128)S(1)} collective-permute-done((f32[8,128]{1,0:T(8,128)S(1)}, f32[8,128]{1,0:T(8,128)S(1)}, u32[]{:S(2)}, u32[]{:S(2)}) %collective-permute-start) | collective-permute-done | bytes 4128 | tf_op jit(solution)/shard_map/ppermute | solution.py:414
  18.3 0.0 copy-done.1
  18.3 0.3 %merge.1 = (f32[2,128]{1,0:T(2,128)S(1)}, f32[2,128]{1,0:T(2,128)S(1)}, f32[16,16]{1,0:T(8,128)S(1)}) custom-call(f32[2,128]{1,0:T(2,128)S(1)} %copy-done.1, f32[8,128]{1,0:T(8,128)S(1)} %stats.1.refs_0_, f32[8,128]{1,0:T(8,128)S(1)} %collective-permute-done.refs_1_, f32[8,128]{1,0:T(8,128)S(1)} %collective-permute-done.1.refs_2_, ...), custom_call_target="tpu_custom_call" | custom-call | tf_op jit(solution)/shard_map/merge/pallas_call | solution.py:418
  18.6 0.0 all-to-all-done
  18.6 0.0 copy-done
  18.6 1.2 %post.1 = (f32[2,128]{1,0:T(2,128)}, bf16[16,16,1280]{2,1,0:T(8,128)(2,1)}) custom-call(f32[64,128]{1,0:T(8,128)S(1)} %bitcast.3, bf16[1280]{0:T(1024)(128)(2,1)S(1)} %copy-done, f32[8,128]{1,0:T(8,128)S(1)} %get-tuple-element.9.local_ref, f32[2,128]{1,0:T(2,128)S(1)} %get-tuple-element.11.logprob_ref, f32[2,128]{1,0:T(2,128)S(1)} %get-tuple-element.12.ratio_ref, ...), custom_call_target="tpu_custom_call" | custom-call | tf_op jit(solution)/shard_map/post/pallas_call | solution.py:431
Async XLA Ops:
  0.6 17.7 %copy-start.1 = (f32[2,128]{1,0:T(2,128)S(1)}, f32[2,128]{1,0:T(2,128)}, u32[]{:S(2)}) copy-start(f32[2,128]{1,0:T(2,128)} %old_ref.1) | copy-start | bytes 3076
  0.6 18.0 %copy-start = (bf16[1280]{0:T(1024)(128)(2,1)S(1)}, bf16[1280]{0:T(1024)(128)(2,1)}, u32[]{:S(2)}) copy-start(bf16[1280]{0:T(1024)(128)(2,1)} %w_ref.1) | copy-start | bytes 7684
  2.7 15.9 %all-to-all-start = ((f32[32,2,128]{2,1,0:T(2,128)}), f32[32,2,128]{2,1,0:T(2,128)S(1)}, u32[]{:S(2)}, u32[]{:S(2)}) async-start(f32[32,2,128]{2,1,0:T(2,128)} %bitcast.1), calls=%async_computation | async-start | bytes 65536 | tf_op jit(solution)/shard_map/all_to_all | solution.py:397
  13.7 2.2 %collective-permute-start.2 = (f32[8,128]{1,0:T(8,128)S(1)}, f32[8,128]{1,0:T(8,128)S(1)}, u32[]{:S(2)}, u32[]{:S(2)}) collective-permute-start(f32[8,128]{1,0:T(8,128)S(1)} %stats.1.refs_0_), channel_id=1, source_target_pairs={{0,1},{1,0},{2,3},{3,2},{4,5},{5,4},{6,7},{7,6},{8,9},{9,8},{10,11... | collective-permute-start | bytes 12296 | tf_op jit(solution)/shard_map/ppermute | solution.py:414
  14.1 2.5 %collective-permute-start.1 = (f32[8,128]{1,0:T(8,128)S(1)}, f32[8,128]{1,0:T(8,128)S(1)}, u32[]{:S(2)}, u32[]{:S(2)}) collective-permute-start(f32[8,128]{1,0:T(8,128)S(1)} %stats.1.refs_0_), channel_id=1, source_target_pairs={{0,2},{1,3},{2,0},{3,1},{4,6},{5,7},{6,4},{7,5},{8,10},{9,11},{10,... | collective-permute-start | bytes 12296 | tf_op jit(solution)/shard_map/ppermute | solution.py:414
  15.3 3.0 %collective-permute-start = (f32[8,128]{1,0:T(8,128)S(1)}, f32[8,128]{1,0:T(8,128)S(1)}, u32[]{:S(2)}, u32[]{:S(2)}) collective-permute-start(f32[8,128]{1,0:T(8,128)S(1)} %stats.1.refs_0_), channel_id=1, source_target_pairs={{0,3},{1,2},{2,1},{3,0},{4,7},{5,6},{6,5},{7,4},{8,11},{9,10},{10,... | collective-permute-start | bytes 12296 | tf_op jit(solution)/shard_map/ppermute | solution.py:414

commit v6 on v5

--- a/solution.py
+++ b/solution.py
@@ -9,6 +9,7 @@
 
 LANES = 128
 STEPS = 4
+NOT_LIVE = 1e9
 F32 = jnp.float32
 
 
@@ -72,7 +73,7 @@
     group, lane, slot = group_grid(dp, tl)
     place = (lane - group * (rows * tl)) & (LANES - 1)
     spot = place // tl
-    blocks = []
+    block = jnp.zeros((dp, LANES), F32)
     for s in range(rows):
         live = live_row(rmask_ref, len_ref, s)
         adv = adv_ref[s : s + 1, :]
@@ -83,17 +84,15 @@
         local_ref[2 * rows + s : 2 * rows + s + 1, :] = adv
         local_ref[3 * rows + s : 3 * rows + s + 1, :] = ret_ref[s : s + 1, :]
         refs = jnp.where(slot == 0, wide_ref[pl.ds(s, dp, stride=rows), :], 0.0)
-        rets = jnp.where(slot == group, jnp.broadcast_to(ret_ref[s : s + 1, :], (dp, LANES)), 0.0)
-        lives = jnp.where(slot == group, jnp.broadcast_to(live, (dp, LANES)), 0.0)
-        block = jnp.where(spot == rows, fold(refs, tl), 0.0)
-        block = jnp.where(spot == rows + 1, fold(rets, tl), block)
-        block = jnp.where(spot == rows + 2, fold(lives, tl), block)
-        last = (rows + 3) * tl
+        rets = jnp.where(live > 0.0, ret_ref[s : s + 1, :], NOT_LIVE)
+        rets = jnp.where(slot == group, jnp.broadcast_to(rets, (dp, LANES)), 0.0)
+        block = jnp.where(spot == rows + s, fold(refs, tl), block)
+        block = jnp.where(spot == 2 * rows + s, fold(rets, tl), block)
+        last = 3 * rows * tl + 4 * s
         block = jnp.where(place == last, jnp.sum(live, axis=1, keepdims=True), block)
         block = jnp.where(place == last + 1, jnp.sum(gain, axis=1, keepdims=True), block)
         block = jnp.where(place == last + 2, jnp.sum(gain * adv, axis=1, keepdims=True), block)
         block = jnp.where(place == last + 3, prompt, block)
-        blocks.append(block)
     for copy in copies[:2]:
         copy.wait()
     weights = w_ref[...][None, :].astype(F32)
@@ -103,13 +102,11 @@
         flat.append(jnp.sum(jnp.transpose(lane_sums(wide)), axis=0, keepdims=True))
     for h in range(rows):
         stats_ref[3 * rows + h : 3 * rows + h + 1, :] = flat[h]
-    for s in range(rows):
-        block = blocks[s]
-        for h in range(rows):
-            line = jnp.broadcast_to(flat[h], (dp, LANES))
-            block = jnp.where((h * LANES + lane) // tl == group * rows + s, line, block)
-        for j in range(tn):
-            send_ref[pl.ds(j * rows + s, dp, stride=tn * rows), :] = block
+    for h in range(rows):
+        line = jnp.broadcast_to(flat[h], (dp, LANES))
+        block = jnp.where((h * LANES + lane) // (rows * tl) == group, line, block)
+    for j in range(tn):
+        send_ref[pl.ds(j, dp, stride=tn), :] = block
     out = pltpu.make_async_copy(send_ref, send_hbm, sems.at[sems.shape[0] - 1])
     out.start()
 
@@ -237,7 +234,6 @@
 def merge_kernel(dims, old_ref, *refs):
     dp, tn, rows, tl = dims
     stats, (logprob_ref, ratio_ref, tile_ref) = refs[:tn], refs[tn:]
-    seqs = dp * rows
     tops = [stat[0:rows, :] for stat in stats]
     row_max = functools.reduce(jnp.maximum, tops)
     exp_sum = sum(
@@ -248,15 +244,14 @@
     logprob_ref[...] = logprob
     ratio_ref[...] = jnp.exp(jnp.clip(logprob - old_ref[...], -20.0, 20.0))
 
-    order = lax.broadcasted_iota(jnp.int32, (seqs, LANES), 0)
-    seq = (order % dp) * rows + order // dp
-    lane = lax.broadcasted_iota(jnp.int32, (seqs, LANES), 1)
-    tile = jnp.zeros((seqs, LANES), F32)
-    for h in range(rows):
-        line = sum(stat[3 * rows + h : 3 * rows + h + 1, :] for stat in stats)
-        here = (h * LANES + lane) // tl == seq
-        tile = jnp.where(here, jnp.broadcast_to(line, (seqs, LANES)), tile)
-    tile_ref[...] = jnp.transpose(fold(tile, tl))[0:tl, :]
+    group, lane, slot = group_grid(dp, tl)
+    for s in range(rows):
+        tile = jnp.zeros((dp, LANES), F32)
+        for h in range(rows):
+            line = sum(stat[3 * rows + h : 3 * rows + h + 1, :] for stat in stats)
+            here = (h * LANES + lane) // tl == group * rows + s
+            tile = jnp.where(here, jnp.broadcast_to(line, (dp, LANES)), tile)
+        tile_ref[s * tl : (s + 1) * tl, :] = jnp.transpose(fold(tile, tl))[0:tl, :]
 
 
 def post_kernel(
@@ -266,46 +261,40 @@
     dp, tn, rows, tl = dims
     seqs = dp * rows
     group, lane, slot = group_grid(dp, tl)
-    parts = [
-        [recv_ref[pl.ds(j * rows + s, dp, stride=tn * rows), :] for j in range(tn)]
-        for s in range(rows)
-    ]
+    parts = [recv_ref[pl.ds(j, dp, stride=tn), :] for j in range(tn)]
     back = LANES - (lax.axis_index("dp") * (rows * tl)) % LANES
-    firsts = [pltpu.roll(part[0], back, 1) for part in parts]
-    every = [pltpu.roll(sum(part[1:], part[0]), back, 1) for part in parts]
+    first = pltpu.roll(parts[0], back, 1)
+    every = pltpu.roll(sum(parts[1:], parts[0]), back, 1)
 
     def row_of(x, k):
         apart = pltpu.roll(x, 0, 1, stride=tl, stride_axis=0)
         row = jnp.sum(jnp.where(slot == (group + k) % dp, apart, 0.0), axis=0, keepdims=True)
         return pltpu.roll(row, LANES - k * tl, 1) if k else row
 
-    spot = (rows + 3) * tl
-    prompts = [first[:, spot + 3 : spot + 4] for first in firsts]
-
-    columns = jnp.transpose(jnp.concatenate(firsts, axis=0))
-    at = (rows + 1) * tl
-    coeff = (
-        32.0 * columns[at + tl : at + 2 * tl, :] * (tile_ref[...] - columns[at : at + tl, :])
-    )
+    targets = jnp.transpose(first)[2 * rows * tl : 3 * rows * tl, :]
+    coeff = jnp.where(targets < 0.5 * NOT_LIVE, 32.0 * (tile_ref[...] - targets), 0.0)
     weights = w_ref[...][None, :].astype(F32)
     pieces = sems.shape[0] - 1
     piece = seqs // pieces
     copies = []
     for k in range(pieces):
         for b in range(k * piece, (k + 1) * piece):
-            at = (b % rows) * dp + b // rows
-            grad_ref[b] = (coeff[:, at : at + 1] * weights).astype(grad_ref.dtype)
+            column = coeff[b % rows * tl : (b % rows + 1) * tl, b // rows : b // rows + 1]
+            grad_ref[b] = (column * weights).astype(grad_ref.dtype)
         at = pl.ds(k * piece, piece)
         copies.append(pltpu.make_async_copy(grad_ref.at[at], grad_hbm.at[at], sems.at[k]))
         copies[-1].start()
 
+    spot = 3 * rows * tl
     for s in range(rows):
-        value_pred = row_of(every[s], s)
-        ref_row = row_of(firsts[s], rows)
+        value_pred = row_of(every, s)
+        ref_row = row_of(first, rows + s)
         own = local_ref[rows + s : rows + s + 1, 0:1]
         sums = jnp.zeros((1, LANES), F32)
-        for first, prompt in zip(firsts, prompts):
-            sums += jnp.sum(jnp.where(prompt == own, first, 0.0), axis=0, keepdims=True)
+        for q in range(rows):
+            same = first[:, spot + 4 * q + 3 : spot + 4 * q + 4] == own
+            part = jnp.sum(jnp.where(same, first, 0.0), axis=0, keepdims=True)
+            sums += pltpu.roll(part, LANES - 4 * q, 1) if q else part
         count = jnp.maximum(sums, 1.0)
         total = pltpu.roll(sums, LANES - 1, 1)
         square = pltpu.roll(sums, LANES - 2, 1)
@@ -345,7 +334,7 @@
     seqs, tl, feat = critic_hidden.shape
     dp, tn = lax.axis_size("dp"), lax.axis_size("tensor")
     dims = (dp, tn, rows, tl)
-    if tokens != LANES or width % LANES or (rows + 3) * tl + 4 > LANES or LANES % tl or tn & (tn - 1):
+    if tokens != LANES or width % LANES or 3 * rows * tl + 4 * rows > LANES or LANES % (rows * tl) or tn & (tn - 1):
         raise ValueError("unsupported shapes")
     vmem = pl.BlockSpec(memory_space=pltpu.VMEM)
     hbm = pl.BlockSpec(memory_space=pltpu.HBM)
@@ -367,7 +356,7 @@
         functools.partial(pre_kernel, dims),
         name="pre",
         out_shape=(
-            jax.ShapeDtypeStruct((dp * tn * rows, LANES), F32),
+            jax.ShapeDtypeStruct((dp * tn, LANES), F32),
             jax.ShapeDtypeStruct((4 * rows, LANES), F32),
             jax.ShapeDtypeStruct((4 * rows, LANES), F32),
         ),
@@ -382,7 +371,7 @@
             pltpu.VMEM((rows, LANES), F32),
             pltpu.VMEM((rows, LANES), jnp.int32),
             pltpu.VMEM((rows, LANES), F32),
-            pltpu.VMEM((dp * tn * rows, LANES), F32),
+            pltpu.VMEM((dp * tn, LANES), F32),
             pltpu.VMEM((seqs, LANES), F32),
             pltpu.SemaphoreType.DMA((max(copies, 8) + 1,)),
             *stats_scratch,
@@ -394,9 +383,7 @@
             returns, response_mask, advantages, token_ids, logits,
         )
     )
-    received = lax.all_to_all(
-        send.reshape(dp * tn, rows, LANES), ("dp", "tensor"), 0, 0, tiled=True
-    ).reshape(dp * tn * rows, LANES)
+    received = lax.all_to_all(send, ("dp", "tensor"), 0, 0, tiled=True)
 
     stats = pl.pallas_call(
         stats_kernel,
@@ -421,7 +408,7 @@
         out_shape=(
             jax.ShapeDtypeStruct((rows, LANES), F32),
             jax.ShapeDtypeStruct((rows, LANES), F32),
-            jax.ShapeDtypeStruct((tl, seqs), F32),
+            jax.ShapeDtypeStruct((rows * tl, dp), F32),
         ),
         in_specs=[vmem] * (1 + tn),
         out_specs=(vmem,) * 3,

time: 20 us -> 20.1 us (level)
  no operation moved by 1% of the time
where the time goes in v6:
time: 20.1 us; the launch traced here: 19.9 us
  starting transfers between devices  8.62 us (43%)
  Pallas kernels  8.13 us (40%)
  waiting for transfers between devices  2.47 us (12%)
  between operations  0.68 us (3%)
    all_to_all x1, starting transfers between devices, per_device(): received = lax.all_to_all(send, ('dp', 'tensor'), 0, 0, tiled=True)  6.41 us
    pallas_call x1, Pallas kernels, per_device(): pl.pallas_call(stats_kernel, name='stats', out_shape=jax.ShapeDtypeStruct...  4.49 us
    ppermute x3, waiting for transfers between devices, per_device(): lax.ppermute(stats, 'tensor', [(t, t ^ k) for t in range(tn)])  2.47 us
    ppermute x3, starting transfers between devices, per_device(): lax.ppermute(stats, 'tensor', [(t, t ^ k) for t in range(tn)])  2.21 us
    pallas_call x1, Pallas kernels, per_device(): pl.pallas_call(functools.partial(pre_kernel, dims), name='pre', out_shape...  2.07 us
    pallas_call x1, Pallas kernels, per_device(): pl.pallas_call(functools.partial(post_kernel, dims), name='post', out_sha...  1.3 us
  transfers between devices with their start and end apart: 4, of which 2 were waited for; matrix products, arithmetic and copies ran while one was open for 0% of the time, Pallas kernels for 24%

profile of v6, /device:TPU:3, one launch (start us, length us, event | category | flops | bytes accessed | tf_op | source)
XLA Modules:
  0.0 19.9 jit_solution(9597121371062747979)
XLA Ops:
  0.6 0.0 copy-start.1
  0.6 0.0 copy-start
  0.7 2.1 %pre.1 = (f32[32,128]{1,0:T(8,128)}, f32[8,128]{1,0:T(8,128)S(1)}, f32[8,128]{1,0:T(8,128)S(1)}) custom-call(s32[2]{0:T(128)} %len_hbm.1, s32[2]{0:T(128)} %prompt_hbm.1, bf16[256,1280]{1,0:T(8,128)(2,1)} %bitcast.6, bf16[1280]{0:T(1024)(128)(2,1)} %w_ref.1, bf16[16,16]{1,0:T(8,128)(2,1)} %refl_hbm.1, f32[2,128]{1,0:T(2,128)} %ret_hbm.1, ...), custom_call_target="tpu_custom_call" | custom-call | tf_op jit(solution)/shard_map/pre/pallas_call | solution.py:355
  2.7 6.4 %all-to-all-start = ((f32[32,1,128]{2,1,0:T(1,128)}), f32[32,1,128]{2,1,0:T(1,128)S(1)}, u32[]{:S(2)}, u32[]{:S(2)}) async-start(f32[32,1,128]{2,1,0:T(1,128)} %bitcast.2), calls=%async_computation | async-start | bytes 32768 | tf_op jit(solution)/shard_map/all_to_all | solution.py:386
  9.2 4.5 %stats.1.refs_0_ = f32[8,128]{1,0:T(8,128)S(1)} custom-call(s32[2,128]{1,0:T(2,128)} %ids_hbm.3, f32[8,128]{1,0:T(8,128)S(1)} %get-tuple-element.10.early_ref, bf16[2,128,4864]{2,1,0:T(8,128)(2,1)} %logits_hbm.3), custom_call_target="tpu_custom_call" | custom-call | flops 9961472 | bytes 2490368 | tf_op jit(solution)/shard_map/stats/pallas_call | solution.py:388
  13.7 0.5 %collective-permute-start.2 = (f32[8,128]{1,0:T(8,128)S(1)}, f32[8,128]{1,0:T(8,128)S(1)}, u32[]{:S(2)}, u32[]{:S(2)}) collective-permute-start(f32[8,128]{1,0:T(8,128)S(1)} %stats.1.refs_0_), channel_id=1, source_target_pairs={{0,1},{1,0},{2,3},{3,2},{4,5},{5,4},{6,7},{7,6},{8,9},{9,8},{10,11... | collective-permute-start | bytes 12296 | tf_op jit(solution)/shard_map/ppermute | solution.py:401
  14.1 1.2 %collective-permute-start.1 = (f32[8,128]{1,0:T(8,128)S(1)}, f32[8,128]{1,0:T(8,128)S(1)}, u32[]{:S(2)}, u32[]{:S(2)}) collective-permute-start(f32[8,128]{1,0:T(8,128)S(1)} %stats.1.refs_0_), channel_id=1, source_target_pairs={{0,2},{1,3},{2,0},{3,1},{4,6},{5,7},{6,4},{7,5},{8,10},{9,11},{10,... | collective-permute-start | bytes 12296 | tf_op jit(solution)/shard_map/ppermute | solution.py:401
  15.3 0.6 %collective-permute-start = (f32[8,128]{1,0:T(8,128)S(1)}, f32[8,128]{1,0:T(8,128)S(1)}, u32[]{:S(2)}, u32[]{:S(2)}) collective-permute-start(f32[8,128]{1,0:T(8,128)S(1)} %stats.1.refs_0_), channel_id=1, source_target_pairs={{0,3},{1,2},{2,1},{3,0},{4,7},{5,6},{6,5},{7,4},{8,11},{9,10},{10,... | collective-permute-start | bytes 12296 | tf_op jit(solution)/shard_map/ppermute | solution.py:401
  15.9 0.0 collective-permute-done.2.refs_3_
  15.9 0.7 %collective-permute-done.1.refs_2_ = f32[8,128]{1,0:T(8,128)S(1)} collective-permute-done((f32[8,128]{1,0:T(8,128)S(1)}, f32[8,128]{1,0:T(8,128)S(1)}, u32[]{:S(2)}, u32[]{:S(2)}) %collective-permute-start.1) | collective-permute-done | bytes 4128 | tf_op jit(solution)/shard_map/ppermute | solution.py:401
  16.6 1.8 %collective-permute-done.refs_1_ = f32[8,128]{1,0:T(8,128)S(1)} collective-permute-done((f32[8,128]{1,0:T(8,128)S(1)}, f32[8,128]{1,0:T(8,128)S(1)}, u32[]{:S(2)}, u32[]{:S(2)}) %collective-permute-start) | collective-permute-done | bytes 4128 | tf_op jit(solution)/shard_map/ppermute | solution.py:401
  18.3 0.0 copy-done.1
  18.3 0.3 %merge.1 = (f32[2,128]{1,0:T(2,128)S(1)}, f32[2,128]{1,0:T(2,128)S(1)}, f32[32,8]{1,0:T(8,128)S(1)}) custom-call(f32[2,128]{1,0:T(2,128)S(1)} %copy-done.1, f32[8,128]{1,0:T(8,128)S(1)} %stats.1.refs_0_, f32[8,128]{1,0:T(8,128)S(1)} %collective-permute-done.refs_1_, f32[8,128]{1,0:T(8,128)S(1)} %collective-permute-done.1.refs_2_, ...), custom_call_target="tpu_custom_call" | custom-call | tf_op jit(solution)/shard_map/merge/pallas_call | solution.py:405
  18.6 0.0 all-to-all-done
  18.6 0.0 copy-done
  18.6 1.3 %post.1 = (f32[2,128]{1,0:T(2,128)}, bf16[16,16,1280]{2,1,0:T(8,128)(2,1)}) custom-call(f32[32,128]{1,0:T(8,128)S(1)} %bitcast.5, bf16[1280]{0:T(1024)(128)(2,1)S(1)} %copy-done, f32[8,128]{1,0:T(8,128)S(1)} %get-tuple-element.9.local_ref, f32[2,128]{1,0:T(2,128)S(1)} %get-tuple-element.11.logprob_ref, f32[2,128]{1,0:T(2,128)S(1)} %get-tuple-element.12.ratio_ref, ...), custom_call_target="tpu_custom_call" | custom-call | tf_op jit(solution)/shard_map/post/pallas_call | solution.py:418
Async XLA Ops:
  0.6 17.7 %copy-start.1 = (f32[2,128]{1,0:T(2,128)S(1)}, f32[2,128]{1,0:T(2,128)}, u32[]{:S(2)}) copy-start(f32[2,128]{1,0:T(2,128)} %old_ref.1) | copy-start | bytes 3076
  0.6 18.0 %copy-start = (bf16[1280]{0:T(1024)(128)(2,1)S(1)}, bf16[1280]{0:T(1024)(128)(2,1)}, u32[]{:S(2)}) copy-start(bf16[1280]{0:T(1024)(128)(2,1)} %w_ref.1) | copy-start | bytes 7684
  2.7 15.9 %all-to-all-start = ((f32[32,1,128]{2,1,0:T(1,128)}), f32[32,1,128]{2,1,0:T(1,128)S(1)}, u32[]{:S(2)}, u32[]{:S(2)}) async-start(f32[32,1,128]{2,1,0:T(1,128)} %bitcast.2), calls=%async_computation | async-start | bytes 32768 | tf_op jit(solution)/shard_map/all_to_all | solution.py:386
  13.7 2.2 %collective-permute-start.2 = (f32[8,128]{1,0:T(8,128)S(1)}, f32[8,128]{1,0:T(8,128)S(1)}, u32[]{:S(2)}, u32[]{:S(2)}) collective-permute-start(f32[8,128]{1,0:T(8,128)S(1)} %stats.1.refs_0_), channel_id=1, source_target_pairs={{0,1},{1,0},{2,3},{3,2},{4,5},{5,4},{6,7},{7,6},{8,9},{9,8},{10,11... | collective-permute-start | bytes 12296 | tf_op jit(solution)/shard_map/ppermute | solution.py:401
  14.1 2.5 %collective-permute-start.1 = (f32[8,128]{1,0:T(8,128)S(1)}, f32[8,128]{1,0:T(8,128)S(1)}, u32[]{:S(2)}, u32[]{:S(2)}) collective-permute-start(f32[8,128]{1,0:T(8,128)S(1)} %stats.1.refs_0_), channel_id=1, source_target_pairs={{0,2},{1,3},{2,0},{3,1},{4,6},{5,7},{6,4},{7,5},{8,10},{9,11},{10,... | collective-permute-start | bytes 12296 | tf_op jit(solution)/shard_map/ppermute | solution.py:401
  15.3 3.0 %collective-permute-start = (f32[8,128]{1,0:T(8,128)S(1)}, f32[8,128]{1,0:T(8,128)S(1)}, u32[]{:S(2)}, u32[]{:S(2)}) collective-permute-start(f32[8,128]{1,0:T(8,128)S(1)} %stats.1.refs_0_), channel_id=1, source_target_pairs={{0,3},{1,2},{2,1},{3,0},{4,7},{5,6},{6,5},{7,4},{8,11},{9,10},{10,... | collective-permute-start | bytes 12296 | tf_op jit(solution)/shard_map/ppermute | solution.py:401
